TPU v7x, 256 devices: a whole 4x4x8 slice. The times are simulated.
256 devices in a mesh: dp: 64 (over z, y, core), mp: 4 (over x).
Axes of the slice: x: 4, y: 4, z: 8, core: 2. Of those that a mesh axis runs over, the one named last changes fastest.
Arguments:
- hidden: bfloat16 [128, 64, 3584], P('dp', None, 'mp'), may hold values from -6 to 6
- rewards: float32 [128, 64], P('dp'), may hold values from -6 to 6
- actions: int32 [128, 64], P('dp'), may hold values from 0 to 152063, as said below
- lengths: int32 [128], P('dp'), may hold values from 1 to 64, 4096 in all
- table: bfloat16 [152064, 3584], P('dp', 'mp'), may hold values from -0.09375 to 0.09375
- q_one: bfloat16 [3584, 3584], P('dp', 'mp'), may hold values from -0.09375 to 0.09375
- q_two: bfloat16 [3584, 3584], P('dp', 'mp'), may hold values from -0.09375 to 0.09375
- t_one: bfloat16 [3584, 3584], P('dp', 'mp'), may hold values from -0.09375 to 0.09375
- t_two: bfloat16 [3584, 3584], P('dp', 'mp'), may hold values from -0.09375 to 0.09375
- value_weight: bfloat16 [3584], P('mp'), may hold values from -0.09375 to 0.09375
- value_bias: float32 [1], replicated, may hold values from -3 to 3
Outputs:
- loss: float32 [], replicated
- grad_q_one: float32 [3584, 3584], P('dp', 'mp')
- grad_q_two: float32 [3584, 3584], P('dp', 'mp')
- grad_value: float32 [3584], P('mp')
- grad_bias: float32 [1], replicated
- target_one: bfloat16 [3584, 3584], P('dp', 'mp')
- target_two: bfloat16 [3584, 3584], P('dp', 'mp')
Inputs may be any that keep to these rules, and one draw needn't show every extreme that they name: `actions`: among the 128 positions of the prompts of one index of dp, exactly 2 action ids fall in each of the aligned blocks of 2376 vocabulary rows.
All inputs are finite; a program needn't handle non-finite values. No bound on the sum of `lengths` on one device may be relied on, other than what follows from the above.
Results may differ from a plain program's by a relative error of at most 0.0045.
Values may be sent and summed in bfloat16 or wider, within the bound.
No kernel may reach another device: no remote copies, remote signals or barrier semaphores. Data moves between devices by JAX's collectives and lax.ppermute only.
A program may use at most 192 MiB of HBM per device.

v0:
```python
import functools

import jax
import jax.numpy as jnp
from jax import lax
from jax.experimental import pallas as pl
from jax.experimental.pallas import tpu as pltpu
from jax.sharding import Mesh
from jax.sharding import PartitionSpec as P


discount = 0.99
expectile = 0.7
polyak_rate = 0.005

ZS, YS, CS, XS = 8, 4, 2, 4
ROWS = ("z", "y", "c")
f32 = jnp.float32
bf16 = jnp.bfloat16
VMEM = pltpu.VMEM
root = 0.7978845608028654
cubic = 0.044715


def exchange(pieces, axes):
    return lax.all_to_all(pieces, axes, split_axis=0, concat_axis=0, tiled=True)


def ahead(a, axis, steps):
    n = lax.axis_size(axis)
    return lax.ppermute(a, axis, tuple(((i + steps) % n, i) for i in range(n)))


def sum_over(a, axis):
    n = lax.axis_size(axis)
    return sum([ahead(a, axis, s) for s in range(1, n)], a)


def split_thrice(a):
    first = a.astype(bf16)
    rest = a - first.astype(f32)
    second = rest.astype(bf16)
    third = (rest - second.astype(f32)).astype(bf16)
    return (first, second, third)


def repack_kernel(place, one, two, three, four, hidden, *outs):
    sent, half_a, half_b, out = outs[:YS], *outs[YS:]
    cols = out.shape[2] // 4
    share = one.shape[0]
    for h, ref in enumerate((one, two, three, four)):
        for y in range(YS):
            out[y, :, h * cols : (h + 1) * cols] = ref[:, y * cols : (y + 1) * cols]
    for r in range(YS):
        sent[r][...] = out[lax.rem(place[0] + YS - r, YS)]
    for half, ref in enumerate((half_a, half_b)):
        for z2 in range(ZS // XS):
            for y in range(YS):
                for c in range(CS):
                    old = ((z2 * YS + y) * CS + c) * share
                    new = ((z2 * CS + c) * YS + y) * share
                    ref[:, new : new + share] = hidden[half, :, old : old + share]


def gather_kernel(place, *refs):
    for r in range(YS):
        refs[YS][lax.rem(place[0] + r, YS)] = refs[r][...]


def forward_kernel(place, *refs):
    a_refs, b_refs = refs[:YS], refs[YS : YS + XS]
    weights, embed_in, extras = refs[YS + XS : YS + XS + 3]
    pre_out, states_out, said = refs[YS + XS + 3 : YS + XS + 6]
    pre, states, embed, held, sems, part_sems, more = refs[YS + XS + 6 :]
    y, x = place[0], place[1]
    slot_count = a_refs[0].shape[1]
    tokens = 2 * slot_count
    heads_width = weights.shape[2]

    def load(xr):
        return pltpu.make_async_copy(weights.at[lax.rem(x + xr, XS)], held.at[xr], sems.at[xr])

    def parts(xr):
        found = []
        for r in range(YS):
            low = pl.ds(r * tokens, slot_count)
            high = pl.ds(r * tokens + slot_count, slot_count)
            for half, (source, to) in enumerate(((a_refs[r].at[xr], low), (b_refs[xr].at[r], high))):
                found.append(
                    pltpu.make_async_copy(source, states.at[xr, to], part_sems.at[xr, r, half])
                )
        return found

    for xr in range(XS):
        load(xr).start()
        for copy in parts(xr):
            copy.start()
    fetch = pltpu.make_async_copy(embed_in, embed, more.at[0])
    fetch.start()
    keep_states = pltpu.make_async_copy(states, states_out, more.at[1])
    for xr in range(XS):
        for copy in parts(xr):
            copy.wait()
        if xr == XS - 1:
            keep_states.start()
        load(xr).wait()

        def columns(at):
            part = jnp.dot(states[xr], held[xr, :, at], preferred_element_type=f32)
            pre[:, at] = part if xr == 0 else pre[:, at] + part

        whole = heads_width // 256

        @pl.loop(0, whole)
        def _(n):
            columns(pl.ds(pl.multiple_of(n * 256, 256), 256))

        if heads_width > whole * 256:
            columns(slice(whole * 256, heads_width))

    cols = heads_width // 4
    keep_pre = pltpu.make_async_copy(pre.at[:, : pre_out.shape[1]], pre_out, more.at[2])
    keep_pre.start()
    fetch.wait()

    @pl.loop(0, YS)
    def _(r):
        rows = pl.ds(pl.multiple_of(r * tokens, tokens), tokens)
        total = extras[...]
        for n in range(heads_width // 128):
            lanes = slice(n * 128, (n + 1) * 128)
            p = pre[rows, lanes]
            g = 0.5 * p * (1.0 + jnp.tanh(root * (p + cubic * (p * p * p))))
            g = g * embed[rows, lanes].astype(f32)
            lane = lax.broadcasted_iota(jnp.int32, (8, 128), 1) + n * 128
            head = lax.broadcasted_iota(jnp.int32, (8, 128), 0)
            chosen = ((lane >= head * cols) & (lane < (head + 1) * cols)).astype(f32).astype(bf16)
            for piece in split_thrice(g):
                total = total + lax.dot_general(
                    chosen, piece, (((1,), (1,)), ((), ())), preferred_element_type=f32
                )
        for copy in range(YS * XS):
            said[copy, lax.rem(y + r, YS)] = total

    keep_states.wait()
    keep_pre.wait()


def backward_kernel(
    place, bias, said, pre_in, embed_in, states_in, keep, send, small, value, *scratch
):
    pre, embed, states, held, grads, sems, more = scratch

    def load(xr):
        return pltpu.make_async_copy(states_in.at[xr], states.at[xr], sems.at[xr])

    fetch_pre = pltpu.make_async_copy(pre_in, pre, more.at[0])
    fetch_embed = pltpu.make_async_copy(embed_in.at[:, : embed.shape[1]], embed, more.at[1])
    fetch_pre.start()
    fetch_embed.start()
    for xr in range(XS):
        load(xr).start()
    y, x, core = place[0], place[1], place[2]
    tokens = said.shape[4]
    width = states.shape[2]
    share = width // (ZS // XS * YS * CS)
    cols = width // YS
    both = 2 * cols
    slot = lax.rem(lax.broadcasted_iota(jnp.int32, (1, tokens), 1), tokens // 2).astype(f32)
    row = lax.broadcasted_iota(jnp.int32, (8, tokens), 0)
    value[...] = jnp.zeros_like(value)
    fetch_pre.wait()
    fetch_embed.wait()
    load(0).wait()

    def prompts(r, sums):
        bias_sum, loss_sum, count_sum = sums
        ya = lax.rem(y + r, YS)
        scores = said[0, 0, ya]
        for i in range(1, YS * XS):
            scores = scores + said[i // XS, i % XS, ya]
        mine = said[ya, 0, 0]
        values = mine[4:5]
        for i in range(1, XS):
            values = values + said[ya, i, 0][4:5]
        values = values + bias[0]
        rewards, length = mine[5:6], mine[6:7]
        valid = slot < length
        following = pltpu.roll(values, tokens - 1, 1)
        target = rewards + discount * jnp.where(slot + 1.0 < length, following, 0.0)
        spread = jnp.minimum(scores[2:3], scores[3:4]) - values
        weights = jnp.where(spread < 0.0, 1.0 - expectile, expectile)
        err_one = scores[0:1] - target
        err_two = scores[1:2] - target
        loss_sum = loss_sum + jnp.where(
            valid, err_one * err_one + err_two * err_two + weights * spread * spread, 0.0
        )
        g_one = jnp.where(valid, 2.0 * err_one, 0.0)
        g_two = jnp.where(valid, 2.0 * err_two, 0.0)
        e = jnp.where(valid, -2.0 * weights * spread, 0.0)
        bias_sum = bias_sum + e
        count_sum = count_sum + jnp.where(slot == 0.0, length, 0.0)
        first = e.astype(bf16).astype(f32)
        second = (e - first).astype(bf16).astype(f32)
        third = e - first - second
        thirds = jnp.where(row == 0, first, jnp.where(row == 1, second, third))
        thirds = jnp.where(row < 3, thirds, 0.0).astype(bf16)
        rows = pl.ds(pl.multiple_of(r * tokens, tokens), tokens)
        value[...] = value[...] + jnp.dot(thirds, states[0, rows], preferred_element_type=f32)
        upright = jnp.transpose(jnp.where(row == 0, g_one, jnp.where(row == 1, g_two, 0.0)))
        left, right = upright[:, 0:1], upright[:, 1:2]
        for n in range(held.shape[1] // 128):
            lanes = slice(n * 128, (n + 1) * 128)
            lane = lax.broadcasted_iota(jnp.int32, (tokens, 128), 1) + n * 128
            g = jnp.where(lane < cols, left, jnp.where(lane < both, right, 0.0))
            p = pre[rows, lanes]
            t = jnp.tanh(root * (p + cubic * (p * p * p)))
            steep = 0.5 * (1.0 + t) + 0.5 * p * (1.0 - t * t) * (
                root * (1.0 + 3.0 * cubic * (p * p))
            )
            held[rows, lanes] = (g * embed[rows, lanes].astype(f32) * steep).astype(bf16)
        return bias_sum, loss_sum, count_sum

    nothing = jnp.zeros((1, tokens), f32)
    bias_sum, loss_sum, count_sum = lax.fori_loop(0, YS, prompts, (nothing, nothing, nothing))
    small[...] = jnp.where(
        row == 0, bias_sum, jnp.where(row == 1, loss_sum, jnp.where(row == 2, count_sum, 0.0))
    )

    @pl.loop(0, XS)
    def _(xr):
        xa = lax.rem(x + xr, XS)

        @pl.when(xr > 0)
        def _():
            load(xr).wait()

        for n in range(held.shape[1] // 256):
            lanes = slice(n * 256, (n + 1) * 256)
            grads[:, lanes] = lax.dot_general(
                states[xr],
                held[:, lanes],
                (((0,), (0,)), ((), ())),
                preferred_element_type=f32,
            )
        for z2 in range(ZS // XS):
            for yy in range(YS):
                to = xa * (ZS // XS) + z2
                low = (z2 * CS * YS + yy) * share
                high = low + YS * share
                for n in range(both // 128):
                    lanes = slice(n * 128, (n + 1) * 128)
                    rows = slice(n * share, (n + 1) * share)
                    first, second = grads[low : low + share, lanes], grads[high : high + share, lanes]
                    keep[to, yy, rows] = jnp.where(core == 0, first, second)
                    send[to, yy, rows] = jnp.where(core == 0, second, first).astype(bf16)
                lanes = slice(both // 128 * 128, both)
                rows = slice(both // 128 * share, None)
                first, second = grads[low : low + share, lanes], grads[high : high + share, lanes]
                mine = jnp.where(core == 0, first, second)
                theirs = jnp.where(core == 0, second, first)
                keep[to, yy, rows] = jnp.concatenate([mine[:32], mine[share - 32 :]], axis=1)
                send[to, yy, rows] = jnp.concatenate(
                    [theirs[:32], theirs[share - 32 :]], axis=1
                ).astype(bf16)


def finish_kernel(*refs):
    totals, landed, one, two, value, rest = refs[:ZS], *refs[ZS:]
    summed = totals[0][...]
    for ref in totals[1:]:
        summed = summed + ref[...]
    factor = 1.0 / jnp.sum(summed[9:10], axis=1, keepdims=True)
    scaled = summed * factor
    value[...] = scaled[:7]
    rest[...] = jnp.broadcast_to(jnp.sum(scaled[7:9], axis=1, keepdims=True), rest.shape)
    share = one.shape[0]
    cols = one.shape[1] // YS
    wide = 2 * cols // 128
    for y in range(YS):
        total = landed[0, y].astype(f32)
        for z in range(1, ZS):
            total = total + landed[z, y].astype(f32)
        total = total * factor
        last = total[wide * share :]
        last = jnp.concatenate([last[: share - 32, :64], last[:, 64:]], axis=0)
        row = jnp.concatenate(
            [total[n * share : (n + 1) * share] for n in range(wide)] + [last], axis=1
        )
        one[:, y * cols : (y + 1) * cols] = row[:, :cols]
        two[:, y * cols : (y + 1) * cols] = row[:, cols:]


def lookup(ids, table, y):
    count = ids.shape[0]
    local_rows = table.shape[0]
    holders = lax.axis_size(ROWS)
    per_holder = count // holders
    columns = table.shape[1] // YS
    place = jnp.arange(count, dtype=jnp.int32)
    holder = ids // local_rows
    local = ids % local_rows
    earlier = (holder[:, None] == holder[None, :]) & (place[None, :] < place[:, None])
    slot = per_holder * holder + jnp.sum(earlier.astype(jnp.int32), axis=1)
    coded = local + 4096 * place
    asked = jnp.sum(jnp.where(slot[:, None] == place[None, :], coded[:, None], 0), axis=0)
    got = exchange(asked.reshape(holders, per_holder), ROWS).reshape(count)
    found = table[got & 4095]
    where = (got >> 12).astype(bf16)
    found = found.reshape(ZS, YS, CS, per_holder, YS, columns).transpose(0, 4, 2, 1, 3, 5)
    where = jnp.broadcast_to(
        where.reshape(ZS, 1, YS, CS, per_holder, 1).transpose(0, 1, 3, 2, 4, 5),
        (ZS, YS, CS, YS, per_holder, 1),
    )
    sent = jnp.concatenate([found, where], axis=-1).reshape(holders, YS * per_holder, columns + 1)
    back = exchange(sent, ROWS)
    back = back.reshape(holders * YS * per_holder, columns + 1)
    slots = jnp.arange(holders * YS * per_holder, dtype=jnp.int32)
    source = (slots // per_holder % YS + YS - y) % YS
    token = source * count + back[:, columns].astype(jnp.int32)
    one_hot = (token[:, None] == jnp.arange(YS * count, dtype=jnp.int32)[None, :]).astype(bf16)
    rows = back[:, :columns]
    return lax.dot_general(
        one_hot,
        jnp.concatenate([rows, rows, rows, rows], axis=1),
        (((0,), (0,)), ((), ())),
        preferred_element_type=f32,
    ).astype(bf16)


def on_device(
    hidden, rewards, actions, lengths, table, q_one, q_two, t_one, t_two, value_weight, value_bias
):
    prompts, slots, width = hidden.shape
    tokens = prompts * slots
    share, head_cols = q_one.shape
    cols = head_cols // YS
    y = lax.axis_index("y")
    place = jnp.stack([y, lax.axis_index("x"), lax.axis_index("c")]).astype(jnp.int32)
    smem = pl.BlockSpec(memory_space=pltpu.SMEM)
    vmem = pl.BlockSpec(memory_space=VMEM)
    anywhere = pl.BlockSpec(memory_space=pl.ANY)
    limit = pltpu.CompilerParams(vmem_limit_bytes=24 * 1024 * 1024)
    near = functools.partial(pltpu.with_memory_space_constraint, memory_space=VMEM)
    far = functools.partial(pltpu.with_memory_space_constraint, memory_space=pltpu.HBM)

    piece = jax.ShapeDtypeStruct((share, 4 * cols), bf16)
    half = jax.ShapeDtypeStruct((slots, width), bf16)
    *sent, half_a, half_b = pl.pallas_call(
        repack_kernel,
        out_shape=(piece,) * YS + (half, half),
        in_specs=[smem] + [vmem] * 5,
        out_specs=(vmem,) * (YS + 2),
        scratch_shapes=[VMEM((YS, share, 4 * cols), bf16)],
    )(place, q_one, q_two, t_one, t_two, hidden)
    pieces = [sent[0]] + [ahead(sent[s], "y", s) for s in range(1, YS)]
    pieces = pl.pallas_call(
        gather_kernel,
        out_shape=jax.ShapeDtypeStruct((YS, share, 4 * cols), bf16),
        in_specs=[smem] + [vmem] * YS,
        out_specs=vmem,
    )(place, *pieces)
    weights = lax.all_gather(pieces.reshape(YS * share, 4 * cols), ("z", "c"), axis=0, tiled=True)
    weights = weights.reshape(XS, width, 4 * cols)
    a_steps = [ahead(half_a, "x", s) for s in range(1, XS)]
    b_steps = [ahead(half_b, "y", s) for s in range(1, YS)]
    a_part = jnp.stack([half_a] + a_steps)
    b_part = jnp.stack([half_b] + b_steps)
    a_parts = [a_part] + [ahead(a_part, "y", s) for s in range(1, YS)]
    b_parts = [b_part] + [ahead(b_part, "x", s) for s in range(1, XS)]
    embed = lookup(actions.reshape(tokens), table, y)

    value_part = jnp.dot(
        hidden.reshape(tokens, width), value_weight, preferred_element_type=f32
    )
    extras = jnp.concatenate(
        [
            jnp.zeros((4, tokens), f32),
            value_part[None],
            rewards.reshape(1, tokens),
            jnp.repeat(lengths.astype(f32), slots)[None],
            jnp.zeros((1, tokens), f32),
        ]
    )
    group = YS * tokens
    pre, states, said = pl.pallas_call(
        forward_kernel,
        out_shape=(
            pltpu.HBM((group, 512), f32),
            pltpu.HBM((XS, group, width), bf16),
            jax.ShapeDtypeStruct((YS * XS, YS, 8, tokens), f32),
        ),
        in_specs=[smem] + [vmem] * (YS + XS) + [anywhere, anywhere, vmem],
        out_specs=(anywhere, anywhere, vmem),
        scratch_shapes=[
            VMEM((group, 4 * cols), f32),
            VMEM((XS, group, width), bf16),
            VMEM((group, 4 * cols), bf16),
            VMEM((XS, width, 4 * cols), bf16),
            pltpu.SemaphoreType.DMA((XS,)),
            pltpu.SemaphoreType.DMA((XS, YS, 2)),
            pltpu.SemaphoreType.DMA((3,)),
        ],
        compiler_params=limit,
        cost_estimate=pl.CostEstimate(
            flops=2 * group * XS * width * 4 * cols, bytes_accessed=12 << 20, transcendentals=0
        ),
    )(place, *map(near, a_parts), *map(near, b_parts), far(weights), far(embed), extras)

    said = exchange(said, ("y", "x")).reshape(YS, XS, YS, 8, tokens)
    packed = (ZS, YS, 3 * share + 32, 128)
    keep, send, small, value = pl.pallas_call(
        backward_kernel,
        out_shape=(
            VMEM(packed, f32),
            VMEM(packed, bf16),
            jax.ShapeDtypeStruct((8, tokens), f32),
            jax.ShapeDtypeStruct((8, width), f32),
        ),
        in_specs=[smem, smem, vmem] + [anywhere] * 3,
        out_specs=(vmem, vmem, vmem, vmem),
        scratch_shapes=[
            VMEM((group, 512), f32),
            VMEM((group, 512), bf16),
            VMEM((XS, group, width), bf16),
            VMEM((group, 512), bf16),
            VMEM((width, 512), f32),
            pltpu.SemaphoreType.DMA((XS,)),
            pltpu.SemaphoreType.DMA((2,)),
        ],
        compiler_params=limit,
        cost_estimate=pl.CostEstimate(
            flops=2 * group * XS * width * 512, bytes_accessed=12 << 20, transcendentals=0
        ),
    )(place, value_bias, near(said), far(pre), far(embed), far(states))
    terms = (keep + ahead(send, "c", 1).astype(f32)).astype(bf16)
    landed = exchange(terms.reshape(ZS * YS, *packed[2:]), ("z", "y")).reshape(packed)

    value = jnp.sum(value[:3], axis=0).reshape(ZS // XS, CS, YS, share)
    value = value.transpose(0, 2, 1, 3).reshape(width)
    totals = jnp.concatenate([value, small[:3].reshape(-1)])
    totals = sum_over(totals.reshape(-1, tokens), "c")
    totals = [totals] + [ahead(totals, "z", s) for s in range(1, ZS)]
    grad_one, grad_two, grad_value, rest = pl.pallas_call(
        finish_kernel,
        out_shape=(
            jax.ShapeDtypeStruct((share, head_cols), f32),
            jax.ShapeDtypeStruct((share, head_cols), f32),
            jax.ShapeDtypeStruct((width // tokens, tokens), f32),
            jax.ShapeDtypeStruct((2, tokens), f32),
        ),
        in_specs=[vmem] * (ZS + 1),
        out_specs=(vmem, vmem, vmem, vmem),
    )(*map(near, totals), near(landed))

    new_one = (
        (1.0 - polyak_rate) * t_one.astype(f32) + polyak_rate * q_one.astype(f32)
    ).astype(bf16)
    new_two = (
        (1.0 - polyak_rate) * t_two.astype(f32) + polyak_rate * q_two.astype(f32)
    ).astype(bf16)
    return (
        rest[1, 0],
        grad_one,
        grad_two,
        grad_value.reshape(width),
        rest[0, :1],
        new_one,
        new_two,
    )


def solution(mesh):
    fine = Mesh(mesh.devices.reshape(ZS, YS, CS, XS), ("z", "y", "c", "x"))
    in_specs = (
        P(ROWS, None, "x"),
        P(ROWS, None),
        P(ROWS, None),
        P(ROWS),
        P(ROWS, "x"),
        P(ROWS, "x"),
        P(ROWS, "x"),
        P(ROWS, "x"),
        P(ROWS, "x"),
        P("x"),
        P(),
    )
    out_specs = (P(), P(ROWS, "x"), P(ROWS, "x"), P("x"), P(), P(ROWS, "x"), P(ROWS, "x"))

    return jax.shard_map(
        on_device, mesh=fine, in_specs=in_specs, out_specs=out_specs, check_vma=False
    )
```

profile of v0, /device:TPU:8, one launch (start us, length us, event | category | flops | bytes accessed | tf_op | source)
XLA Modules:
  0.0 198.4 jit_solution(10175905017152192066)
XLA Ops:
  7.8 2.2 %shard_map.162 = (bf16[56,896]{1,0:T(8,128)(2,1)}, bf16[56,896]{1,0:T(8,128)(2,1)}, bf16[56,896]{1,0:T(8,128)(2,1)}, bf16[56,896]{1,0:T(8,128)(2,1)}, bf16[64,896]{1,0:T(8,128)(2,1)}, /*index=5*/bf16[64,896]{1,0:T(8,128)(2,1)}) custom-call(s32[3]{0:T(128)} %pad_add_fusion.place, bf16[56,896]{1,0:T(8,128)(2,1)} %one.1, bf16[56,896]{1,0:T(8,128)(2,1)} %two.1, ...), custom_call_target="tpu_custom_call" | custom-call | tf_op jit(solution)/shard_map/pallas_call | solution.py:349
  10.1 2.2 %collective-permute-start.12 = (bf16[56,896]{1,0:T(8,128)(2,1)}, bf16[56,896]{1,0:T(8,128)(2,1)S(1)}, u32[]{:S(2)}, u32[]{:S(2)}) collective-permute-start(bf16[56,896]{1,0:T(8,128)(2,1)} %get-tuple-element.27), channel_id=1, source_target_pairs={{8,0},{16,8},{24,16},{0,24},{9,1},{17,9},{25,17},{1,25},{10,2},{18... | collective-permute-start | bytes 301064 | tf_op jit(solution)/shard_map/ppermute | solution.py:31
  13.1 1.9 collective-permute-start.14
  15.2 3.3 %collective-permute-done.13.refs_2_ = bf16[56,896]{1,0:T(8,128)(2,1)S(1)} collective-permute-done((bf16[56,896]{1,0:T(8,128)(2,1)}, bf16[56,896]{1,0:T(8,128)(2,1)S(1)}, u32[]{:S(2)}, u32[]{:S(2)}) %collective-permute-start.13) | collective-permute-done | bytes 100384 | tf_op jit(solution)/shard_map/ppermute | solution.py:31
  19.4 1.8 shard_map.163
  22.7 12.0 %all-to-all-start = ((s32[64,1,2]{2,1,0:T(1,128)}), s32[64,1,2]{2,1,0:T(1,128)S(1)}, u32[]{:S(2)}, u32[]{:S(2)}) async-start(s32[64,1,2]{2,1,0:T(1,128)} %bitcast.13), calls=%async_computation | async-start | bytes 65536 | tf_op jit(solution)/shard_map/all_to_all | solution.py:26
  34.7 1.5 collective-permute-start.8
  36.8 2.1 %collective-permute-start.7 = (bf16[64,896]{1,0:T(8,128)(2,1)}, bf16[64,896]{1,0:T(8,128)(2,1)S(1)}, u32[]{:S(2)}, u32[]{:S(2)}) collective-permute-start(bf16[64,896]{1,0:T(8,128)(2,1)} %get-tuple-element.25), channel_id=1, source_target_pairs={{16,0},{24,8},{0,16},{8,24},{17,1},{25,9},{1,17},{9,25},{18,2},{26... | collective-permute-start | bytes 344072 | tf_op jit(solution)/shard_map/ppermute | solution.py:31
  38.9 4.5 %all-to-all-done = s32[64,1,2]{2,1,0:T(1,128)S(1)} async-done(((s32[64,1,2]{2,1,0:T(1,128)}), s32[64,1,2]{2,1,0:T(1,128)S(1)}, u32[]{:S(2)}, u32[]{:S(2)}) %all-to-all-start) | async-done | bytes 544 | tf_op jit(solution)/shard_map/all_to_all | solution.py:26
  43.6 3.9 %gather_fusion = bf16[128,896]{1,0:T(8,128)(2,1)S(1)} fusion(bf16[2376,896]{1,0:T(8,128)(2,1)} %param.15, s32[1024]{0:T(1024)S(1)} %pad_clamp_fusion), kind=kCustom, calls=%fused_computation | custom fusion | bytes 459264 | tf_op jit(solution)/shard_map/gather | solution.py:308
  48.6 3.1 %collective-permute-start.10 = (bf16[4,64,896]{2,1,0:T(8,128)(2,1)S(1)}, bf16[4,64,896]{2,1,0:T(8,128)(2,1)S(1)}, u32[]{:S(2)}, u32[]{:S(2)}) collective-permute-start(bf16[4,64,896]{2,1,0:T(8,128)(2,1)S(1)} %pad_maximum_fusion.1.refs_4_), channel_id=1, source_target_pairs={{2,0},{3,1},{0,2},{1,3},{6,4},{7,5},{4,6},{5,7},{10,8},{11,9},{8,1... | collective-permute-start | bytes 1376264 | tf_op jit(solution)/shard_map/ppermute | solution.py:31
  53.3 5.6 %all-to-all-start.1 = ((bf16[64,8,225]{2,1,0:T(8,128)(2,1)}), bf16[64,8,225]{2,1,0:T(8,128)(2,1)S(1)}, u32[]{:S(2)}, u32[]{:S(2)}) async-start(bf16[64,8,225]{2,1,0:T(8,128)(2,1)} %reshape.285), calls=%async_computation.1 | async-start | bytes 524288 | tf_op jit(solution)/shard_map/all_to_all | solution.py:26
  60.1 1.5 collective-permute-start.1
  62.1 2.0 %collective-permute-start.11 = (bf16[4,64,896]{2,1,0:T(8,128)(2,1)S(1)}, bf16[4,64,896]{2,1,0:T(8,128)(2,1)S(1)}, u32[]{:S(2)}, u32[]{:S(2)}) collective-permute-start(bf16[4,64,896]{2,1,0:T(8,128)(2,1)S(1)} %pad_maximum_fusion.1.refs_4_), channel_id=1, source_target_pairs={{3,0},{0,1},{1,2},{2,3},{7,4},{4,5},{5,6},{6,7},{11,8},{8,9},{9,10... | collective-permute-start | bytes 1376264 | tf_op jit(solution)/shard_map/ppermute | solution.py:31
  64.2 1.7 collective-permute-done
  65.9 2.7 %collective-permute-start.9 = (bf16[4,64,896]{2,1,0:T(8,128)(2,1)S(1)}, bf16[4,64,896]{2,1,0:T(8,128)(2,1)S(1)}, u32[]{:S(2)}, u32[]{:S(2)}) collective-permute-start(bf16[4,64,896]{2,1,0:T(8,128)(2,1)S(1)} %pad_maximum_fusion.1.refs_4_), channel_id=1, source_target_pairs={{1,0},{2,1},{3,2},{0,3},{5,4},{6,5},{7,6},{4,7},{9,8},{10,9},{11,1... | collective-permute-start | bytes 1376264 | tf_op jit(solution)/shard_map/ppermute | solution.py:31
  70.4 2.1 %collective-permute-start.4 = (bf16[4,64,896]{2,1,0:T(8,128)(2,1)S(1)}, bf16[4,64,896]{2,1,0:T(8,128)(2,1)S(1)}, u32[]{:S(2)}, u32[]{:S(2)}) collective-permute-start(bf16[4,64,896]{2,1,0:T(8,128)(2,1)S(1)} %pad_maximum_fusion.refs_0_), channel_id=1, source_target_pairs={{16,0},{24,8},{0,16},{8,24},{17,1},{25,9},{1,17},{9,25},{18,2},{26... | collective-permute-start | bytes 1376264 | tf_op jit(solution)/shard_map/ppermute | solution.py:31
  75.8 1.5 collective-permute-start.5
  77.4 2.0 %convolution_convert_fusion.refs_9_.embed_in = bf16[512,896]{1,0:T(8,128)(2,1)} fusion(bf16[512,224]{1,0:T(8,128)(2,1)S(1)} %bitcast.50, s32[512]{0:T(512)S(1)} %bitcast.61), kind=kOutput, calls=%fused_computation.2 | convolution fusion | flops 474152960 | bytes 1148928 | tf_op jit(solution)/shard_map/dot_general | solution.py:323
  79.4 2.9 %collective-permute-done.3.refs_1_ = bf16[4,64,896]{2,1,0:T(8,128)(2,1)S(1)} collective-permute-done((bf16[4,64,896]{2,1,0:T(8,128)(2,1)S(1)}, bf16[4,64,896]{2,1,0:T(8,128)(2,1)S(1)}, u32[]{:S(2)}, u32[]{:S(2)}) %collective-permute-start.3) | collective-permute-done | bytes 458784 | tf_op jit(solution)/shard_map/ppermute | solution.py:31
  82.4 9.9 %collective-permute-done.4.refs_2_ = bf16[4,64,896]{2,1,0:T(8,128)(2,1)S(1)} collective-permute-done((bf16[4,64,896]{2,1,0:T(8,128)(2,1)S(1)}, bf16[4,64,896]{2,1,0:T(8,128)(2,1)S(1)}, u32[]{:S(2)}, u32[]{:S(2)}) %collective-permute-start.4) | collective-permute-done | bytes 458784 | tf_op jit(solution)/shard_map/ppermute | solution.py:31
  94.7 15.5 %shard_map.164 = (f32[512,512]{1,0:T(8,128)}, bf16[4,512,896]{2,1,0:T(8,128)(2,1)}, f32[16,4,8,128]{3,2,1,0:T(8,128)}) custom-call(s32[3]{0:T(128)S(1)} %copy-done, bf16[4,64,896]{2,1,0:T(8,128)(2,1)S(1)} %pad_maximum_fusion.refs_0_, bf16[4,64,896]{2,1,0:T(8,128)(2,1)S(1)} %collective-permute-done.3.refs_1_, ...), custom_call_target="tpu_custom_call" | custom-call | flops 3288334336 | bytes 12582912 | tf_op jit(solution)/shard_map/pallas_call | solution.py:386
  110.2 6.1 %all-to-all-start.2 = ((f32[16,4,8,128]{3,2,1,0:T(8,128)}), f32[16,4,8,128]{3,2,1,0:T(8,128)S(1)}, u32[]{:S(2)}, u32[]{:S(2)}) async-start(f32[16,4,8,128]{3,2,1,0:T(8,128)} %get-tuple-element.30), calls=%async_computation.2 | async-start | bytes 524288 | tf_op jit(solution)/shard_map/all_to_all | solution.py:26
  116.9 6.7 %all-to-all-done.2 = f32[16,4,8,128]{3,2,1,0:T(8,128)S(1)} async-done(((f32[16,4,8,128]{3,2,1,0:T(8,128)}), f32[16,4,8,128]{3,2,1,0:T(8,128)S(1)}, u32[]{:S(2)}, u32[]{:S(2)}) %all-to-all-start.2) | async-done | bytes 262176 | tf_op jit(solution)/shard_map/all_to_all | solution.py:26
  123.6 7.1 %shard_map.165 = (f32[8,4,200,128]{3,2,1,0:T(8,128)S(1)}, bf16[8,4,200,128]{3,2,1,0:T(8,128)(2,1)S(1)}, f32[8,128]{1,0:T(8,128)S(1)}, f32[8,896]{1,0:T(8,128)S(1)}) custom-call(s32[3]{0:T(128)S(1)} %copy-done, f32[1]{0:T(128)S(6)} %copy.58.bias, f32[4,4,4,8,128]{4,3,2,1,0:T(8,128)S(1)} %bitcast.45, f32[512,512]{1,0:T(8,128)} %get-tuple-element.31.pre_in, ...), custom_call_target="tpu_custom_call" | custom-call | flops 1879048192 | bytes 12582912 | tf_op jit(solution)/shard_map/pallas_call | solution.py:412
  130.9 3.5 %collective-permute-done.23 = bf16[8,4,200,128]{3,2,1,0:T(8,128)(2,1)S(1)} collective-permute-done((bf16[8,4,200,128]{3,2,1,0:T(8,128)(2,1)S(1)}, bf16[8,4,200,128]{3,2,1,0:T(8,128)(2,1)S(1)}, u32[]{:S(2)}, u32[]{:S(2)}) %collective-permute-start.23) | collective-permute-done | bytes 1638432 | tf_op jit(solution)/shard_map/ppermute | solution.py:31
  135.9 9.3 %all-to-all-start.3 = ((bf16[32,200,128]{2,1,0:T(8,128)(2,1)}), bf16[32,200,128]{2,1,0:T(8,128)(2,1)S(1)}, u32[]{:S(2)}, u32[]{:S(2)}) async-start(bf16[32,200,128]{2,1,0:T(8,128)(2,1)} %bitcast.26), calls=%async_computation.3 | async-start | bytes 3276800 | tf_op jit(solution)/shard_map/all_to_all | solution.py:26
  146.7 2.8 %collective-permute-start.16 = (f32[10,128]{1,0:T(8,128)S(1)}, f32[10,128]{1,0:T(8,128)S(1)}, u32[]{:S(2)}, u32[]{:S(2)}) collective-permute-start(f32[10,128]{1,0:T(8,128)S(1)} %fusion.18.refs_0_), channel_id=1, source_target_pairs={{32,0},{64,32},{96,64},{128,96},{160,128},{192,160},{224,192},{0,2... | collective-permute-start | bytes 15368 | tf_op jit(solution)/shard_map/ppermute | solution.py:31
  149.5 2.3 %collective-permute-start.17 = (f32[10,128]{1,0:T(8,128)S(1)}, f32[10,128]{1,0:T(8,128)S(1)}, u32[]{:S(2)}, u32[]{:S(2)}) collective-permute-start(f32[10,128]{1,0:T(8,128)S(1)} %fusion.18.refs_0_), channel_id=1, source_target_pairs={{64,0},{96,32},{128,64},{160,96},{192,128},{224,160},{0,192},{32,2... | collective-permute-start | bytes 15368 | tf_op jit(solution)/shard_map/ppermute | solution.py:31
  153.2 3.6 %collective-permute-start.19 = (f32[10,128]{1,0:T(8,128)S(1)}, f32[10,128]{1,0:T(8,128)S(1)}, u32[]{:S(2)}, u32[]{:S(2)}) collective-permute-start(f32[10,128]{1,0:T(8,128)S(1)} %fusion.18.refs_0_), channel_id=1, source_target_pairs={{128,0},{160,32},{192,64},{224,96},{0,128},{32,160},{64,192},{96,2... | collective-permute-start | bytes 15368 | tf_op jit(solution)/shard_map/ppermute | solution.py:31
  157.0 26.4 %collective-permute-done.16.refs_1_ = f32[10,128]{1,0:T(8,128)S(1)} collective-permute-done((f32[10,128]{1,0:T(8,128)S(1)}, f32[10,128]{1,0:T(8,128)S(1)}, u32[]{:S(2)}, u32[]{:S(2)}) %collective-permute-start.16) | collective-permute-done | bytes 5152 | tf_op jit(solution)/shard_map/ppermute | solution.py:31
  183.4 4.2 %collective-permute-start.22 = (f32[10,128]{1,0:T(8,128)S(1)}, f32[10,128]{1,0:T(8,128)S(1)}, u32[]{:S(2)}, u32[]{:S(2)}) collective-permute-start(f32[10,128]{1,0:T(8,128)S(1)} %fusion.18.refs_0_), channel_id=1, source_target_pairs={{224,0},{0,32},{32,64},{64,96},{96,128},{128,160},{160,192},{192,2... | collective-permute-start | bytes 15368 | tf_op jit(solution)/shard_map/ppermute | solution.py:31
  (116 shorter events, 25.4 us)
Async XLA Ops:
  7.2 86.5 %all-gather.2.cloned.1.call-start = ((), (), s32[]{:S(2)}) async-start(), calls=%async_computation.4 | async-start | bytes 6823936 | tf_op jit(solution)/shard_map/all_gather | solution.py:363
  10.1 5.2 %collective-permute-start.12 = (bf16[56,896]{1,0:T(8,128)(2,1)}, bf16[56,896]{1,0:T(8,128)(2,1)S(1)}, u32[]{:S(2)}, u32[]{:S(2)}) collective-permute-start(bf16[56,896]{1,0:T(8,128)(2,1)} %get-tuple-element.27), channel_id=1, source_target_pairs={{8,0},{16,8},{24,16},{0,24},{9,1},{17,9},{25,17},{1,25},{10,2},{18... | collective-permute-start | bytes 301064 | tf_op jit(solution)/shard_map/ppermute | solution.py:31
  12.2 6.4 %collective-permute-start.13 = (bf16[56,896]{1,0:T(8,128)(2,1)}, bf16[56,896]{1,0:T(8,128)(2,1)S(1)}, u32[]{:S(2)}, u32[]{:S(2)}) collective-permute-start(bf16[56,896]{1,0:T(8,128)(2,1)} %get-tuple-element.28), channel_id=1, source_target_pairs={{16,0},{24,8},{0,16},{8,24},{17,1},{25,9},{1,17},{9,25},{18,2},{26... | collective-permute-start | bytes 301064 | tf_op jit(solution)/shard_map/ppermute | solution.py:31
  13.1 5.7 %collective-permute-start.14 = (bf16[56,896]{1,0:T(8,128)(2,1)}, bf16[56,896]{1,0:T(8,128)(2,1)S(1)}, u32[]{:S(2)}, u32[]{:S(2)}) collective-permute-start(bf16[56,896]{1,0:T(8,128)(2,1)} %get-tuple-element.29), channel_id=1, source_target_pairs={{24,0},{0,8},{8,16},{16,24},{25,1},{1,9},{9,17},{17,25},{26,2},{2,... | collective-permute-start | bytes 301064 | tf_op jit(solution)/shard_map/ppermute | solution.py:31
  22.7 20.7 %all-to-all-start = ((s32[64,1,2]{2,1,0:T(1,128)}), s32[64,1,2]{2,1,0:T(1,128)S(1)}, u32[]{:S(2)}, u32[]{:S(2)}) async-start(s32[64,1,2]{2,1,0:T(1,128)} %bitcast.13), calls=%async_computation | async-start | bytes 65536 | tf_op jit(solution)/shard_map/all_to_all | solution.py:26
  34.7 13.8 %collective-permute-start.8 = (bf16[64,896]{1,0:T(8,128)(2,1)}, bf16[64,896]{1,0:T(8,128)(2,1)S(1)}, u32[]{:S(2)}, u32[]{:S(2)}) collective-permute-start(bf16[64,896]{1,0:T(8,128)(2,1)} %get-tuple-element.25), channel_id=1, source_target_pairs={{24,0},{0,8},{8,16},{16,24},{25,1},{1,9},{9,17},{17,25},{26,2},{2,... | collective-permute-start | bytes 344072 | tf_op jit(solution)/shard_map/ppermute | solution.py:31
  36.2 12.3 %collective-permute-start.6 = (bf16[64,896]{1,0:T(8,128)(2,1)}, bf16[64,896]{1,0:T(8,128)(2,1)S(1)}, u32[]{:S(2)}, u32[]{:S(2)}) collective-permute-start(bf16[64,896]{1,0:T(8,128)(2,1)} %get-tuple-element.25), channel_id=1, source_target_pairs={{8,0},{16,8},{24,16},{0,24},{9,1},{17,9},{25,17},{1,25},{10,2},{18... | collective-permute-start | bytes 344072 | tf_op jit(solution)/shard_map/ppermute | solution.py:31
  36.8 11.7 %collective-permute-start.7 = (bf16[64,896]{1,0:T(8,128)(2,1)}, bf16[64,896]{1,0:T(8,128)(2,1)S(1)}, u32[]{:S(2)}, u32[]{:S(2)}) collective-permute-start(bf16[64,896]{1,0:T(8,128)(2,1)} %get-tuple-element.25), channel_id=1, source_target_pairs={{16,0},{24,8},{0,16},{8,24},{17,1},{25,9},{1,17},{9,25},{18,2},{26... | collective-permute-start | bytes 344072 | tf_op jit(solution)/shard_map/ppermute | solution.py:31
  48.6 27.2 %collective-permute-start.10 = (bf16[4,64,896]{2,1,0:T(8,128)(2,1)S(1)}, bf16[4,64,896]{2,1,0:T(8,128)(2,1)S(1)}, u32[]{:S(2)}, u32[]{:S(2)}) collective-permute-start(bf16[4,64,896]{2,1,0:T(8,128)(2,1)S(1)} %pad_maximum_fusion.1.refs_4_), channel_id=1, source_target_pairs={{2,0},{3,1},{0,2},{1,3},{6,4},{7,5},{4,6},{5,7},{10,8},{11,9},{8,1... | collective-permute-start | bytes 1376264 | tf_op jit(solution)/shard_map/ppermute | solution.py:31
  53.3 20.7 %all-to-all-start.1 = ((bf16[64,8,225]{2,1,0:T(8,128)(2,1)}), bf16[64,8,225]{2,1,0:T(8,128)(2,1)S(1)}, u32[]{:S(2)}, u32[]{:S(2)}) async-start(bf16[64,8,225]{2,1,0:T(8,128)(2,1)} %reshape.285), calls=%async_computation.1 | async-start | bytes 524288 | tf_op jit(solution)/shard_map/all_to_all | solution.py:26
  58.9 7.0 %collective-permute-start = (bf16[64,896]{1,0:T(8,128)(2,1)S(1)}, bf16[64,896]{1,0:T(8,128)(2,1)S(1)}, u32[]{:S(2)}, u32[]{:S(2)}) collective-permute-start(bf16[64,896]{1,0:T(8,128)(2,1)S(1)} %copy-done.8), channel_id=1, source_target_pairs={{1,0},{2,1},{3,2},{0,3},{5,4},{6,5},{7,6},{4,7},{9,8},{10,9},{11,1... | collective-permute-start | bytes 344072 | tf_op jit(solution)/shard_map/ppermute | solution.py:31
  60.1 8.5 %collective-permute-start.1 = (bf16[64,896]{1,0:T(8,128)(2,1)S(1)}, bf16[64,896]{1,0:T(8,128)(2,1)S(1)}, u32[]{:S(2)}, u32[]{:S(2)}) collective-permute-start(bf16[64,896]{1,0:T(8,128)(2,1)S(1)} %copy-done.8), channel_id=1, source_target_pairs={{2,0},{3,1},{0,2},{1,3},{6,4},{7,5},{4,6},{5,7},{10,8},{11,9},{8,1... | collective-permute-start | bytes 344072 | tf_op jit(solution)/shard_map/ppermute | solution.py:31
  61.6 7.8 %collective-permute-start.2 = (bf16[64,896]{1,0:T(8,128)(2,1)S(1)}, bf16[64,896]{1,0:T(8,128)(2,1)S(1)}, u32[]{:S(2)}, u32[]{:S(2)}) collective-permute-start(bf16[64,896]{1,0:T(8,128)(2,1)S(1)} %copy-done.8), channel_id=1, source_target_pairs={{3,0},{0,1},{1,2},{2,3},{7,4},{4,5},{5,6},{6,7},{11,8},{8,9},{9,10... | collective-permute-start | bytes 344072 | tf_op jit(solution)/shard_map/ppermute | solution.py:31
  62.1 17.3 %collective-permute-start.11 = (bf16[4,64,896]{2,1,0:T(8,128)(2,1)S(1)}, bf16[4,64,896]{2,1,0:T(8,128)(2,1)S(1)}, u32[]{:S(2)}, u32[]{:S(2)}) collective-permute-start(bf16[4,64,896]{2,1,0:T(8,128)(2,1)S(1)} %pad_maximum_fusion.1.refs_4_), channel_id=1, source_target_pairs={{3,0},{0,1},{1,2},{2,3},{7,4},{4,5},{5,6},{6,7},{11,8},{8,9},{9,10... | collective-permute-start | bytes 1376264 | tf_op jit(solution)/shard_map/ppermute | solution.py:31
  65.9 13.5 %collective-permute-start.9 = (bf16[4,64,896]{2,1,0:T(8,128)(2,1)S(1)}, bf16[4,64,896]{2,1,0:T(8,128)(2,1)S(1)}, u32[]{:S(2)}, u32[]{:S(2)}) collective-permute-start(bf16[4,64,896]{2,1,0:T(8,128)(2,1)S(1)} %pad_maximum_fusion.1.refs_4_), channel_id=1, source_target_pairs={{1,0},{2,1},{3,2},{0,3},{5,4},{6,5},{7,6},{4,7},{9,8},{10,9},{11,1... | collective-permute-start | bytes 1376264 | tf_op jit(solution)/shard_map/ppermute | solution.py:31
  69.6 12.8 %collective-permute-start.3 = (bf16[4,64,896]{2,1,0:T(8,128)(2,1)S(1)}, bf16[4,64,896]{2,1,0:T(8,128)(2,1)S(1)}, u32[]{:S(2)}, u32[]{:S(2)}) collective-permute-start(bf16[4,64,896]{2,1,0:T(8,128)(2,1)S(1)} %pad_maximum_fusion.refs_0_), channel_id=1, source_target_pairs={{8,0},{16,8},{24,16},{0,24},{9,1},{17,9},{25,17},{1,25},{10,2},{18... | collective-permute-start | bytes 1376264 | tf_op jit(solution)/shard_map/ppermute | solution.py:31
  70.4 21.8 %collective-permute-start.4 = (bf16[4,64,896]{2,1,0:T(8,128)(2,1)S(1)}, bf16[4,64,896]{2,1,0:T(8,128)(2,1)S(1)}, u32[]{:S(2)}, u32[]{:S(2)}) collective-permute-start(bf16[4,64,896]{2,1,0:T(8,128)(2,1)S(1)} %pad_maximum_fusion.refs_0_), channel_id=1, source_target_pairs={{16,0},{24,8},{0,16},{8,24},{17,1},{25,9},{1,17},{9,25},{18,2},{26... | collective-permute-start | bytes 1376264 | tf_op jit(solution)/shard_map/ppermute | solution.py:31
  75.8 17.1 %collective-permute-start.5 = (bf16[4,64,896]{2,1,0:T(8,128)(2,1)S(1)}, bf16[4,64,896]{2,1,0:T(8,128)(2,1)S(1)}, u32[]{:S(2)}, u32[]{:S(2)}) collective-permute-start(bf16[4,64,896]{2,1,0:T(8,128)(2,1)S(1)} %pad_maximum_fusion.refs_0_), channel_id=1, source_target_pairs={{24,0},{0,8},{8,16},{16,24},{25,1},{1,9},{9,17},{17,25},{26,2},{2,... | collective-permute-start | bytes 1376264 | tf_op jit(solution)/shard_map/ppermute | solution.py:31
  110.2 13.4 %all-to-all-start.2 = ((f32[16,4,8,128]{3,2,1,0:T(8,128)}), f32[16,4,8,128]{3,2,1,0:T(8,128)S(1)}, u32[]{:S(2)}, u32[]{:S(2)}) async-start(f32[16,4,8,128]{3,2,1,0:T(8,128)} %get-tuple-element.30), calls=%async_computation.2 | async-start | bytes 524288 | tf_op jit(solution)/shard_map/all_to_all | solution.py:26
  130.8 3.6 %collective-permute-start.23 = (bf16[8,4,200,128]{3,2,1,0:T(8,128)(2,1)S(1)}, bf16[8,4,200,128]{3,2,1,0:T(8,128)(2,1)S(1)}, u32[]{:S(2)}, u32[]{:S(2)}) collective-permute-start(bf16[8,4,200,128]{3,2,1,0:T(8,128)(2,1)S(1)} %get-tuple-element.36), channel_id=1, source_target_pairs={{4,0},{0,4},{5,1},{1,5},{6,2},{2,6},{7,3},{3,7},{12,8},{8,12},{13,... | collective-permute-start | bytes 4915208 | tf_op jit(solution)/shard_map/ppermute | solution.py:31
  135.9 51.7 %copy-start.5 = (bf16[56,896]{1,0:T(8,128)(2,1)S(1)}, bf16[56,896]{1,0:T(8,128)(2,1)}, u32[]{:S(2)}) copy-start(bf16[56,896]{1,0:T(8,128)(2,1)} %two.1) | copy-start | bytes 301060
  135.9 51.7 %copy-start.6 = (bf16[56,896]{1,0:T(8,128)(2,1)S(1)}, bf16[56,896]{1,0:T(8,128)(2,1)}, u32[]{:S(2)}) copy-start(bf16[56,896]{1,0:T(8,128)(2,1)} %three.1) | copy-start | bytes 301060
  135.9 51.7 %copy-start.7 = (bf16[56,896]{1,0:T(8,128)(2,1)S(1)}, bf16[56,896]{1,0:T(8,128)(2,1)}, u32[]{:S(2)}) copy-start(bf16[56,896]{1,0:T(8,128)(2,1)} %four.1) | copy-start | bytes 301060
  135.9 53.3 %all-to-all-start.3 = ((bf16[32,200,128]{2,1,0:T(8,128)(2,1)}), bf16[32,200,128]{2,1,0:T(8,128)(2,1)S(1)}, u32[]{:S(2)}, u32[]{:S(2)}) async-start(bf16[32,200,128]{2,1,0:T(8,128)(2,1)} %bitcast.26), calls=%async_computation.3 | async-start | bytes 3276800 | tf_op jit(solution)/shard_map/all_to_all | solution.py:26
  145.4 1.3 collective-permute-start.15
  146.7 36.7 %collective-permute-start.16 = (f32[10,128]{1,0:T(8,128)S(1)}, f32[10,128]{1,0:T(8,128)S(1)}, u32[]{:S(2)}, u32[]{:S(2)}) collective-permute-start(f32[10,128]{1,0:T(8,128)S(1)} %fusion.18.refs_0_), channel_id=1, source_target_pairs={{32,0},{64,32},{96,64},{128,96},{160,128},{192,160},{224,192},{0,2... | collective-permute-start | bytes 15368 | tf_op jit(solution)/shard_map/ppermute | solution.py:31
  149.5 34.0 %collective-permute-start.17 = (f32[10,128]{1,0:T(8,128)S(1)}, f32[10,128]{1,0:T(8,128)S(1)}, u32[]{:S(2)}, u32[]{:S(2)}) collective-permute-start(f32[10,128]{1,0:T(8,128)S(1)} %fusion.18.refs_0_), channel_id=1, source_target_pairs={{64,0},{96,32},{128,64},{160,96},{192,128},{224,160},{0,192},{32,2... | collective-permute-start | bytes 15368 | tf_op jit(solution)/shard_map/ppermute | solution.py:31
  151.8 36.6 %collective-permute-start.18 = (f32[10,128]{1,0:T(8,128)S(1)}, f32[10,128]{1,0:T(8,128)S(1)}, u32[]{:S(2)}, u32[]{:S(2)}) collective-permute-start(f32[10,128]{1,0:T(8,128)S(1)} %fusion.18.refs_0_), channel_id=1, source_target_pairs={{96,0},{128,32},{160,64},{192,96},{224,128},{0,160},{32,192},{64,2... | collective-permute-start | bytes 15368 | tf_op jit(solution)/shard_map/ppermute | solution.py:31
  153.2 35.2 %collective-permute-start.19 = (f32[10,128]{1,0:T(8,128)S(1)}, f32[10,128]{1,0:T(8,128)S(1)}, u32[]{:S(2)}, u32[]{:S(2)}) collective-permute-start(f32[10,128]{1,0:T(8,128)S(1)} %fusion.18.refs_0_), channel_id=1, source_target_pairs={{128,0},{160,32},{192,64},{224,96},{0,128},{32,160},{64,192},{96,2... | collective-permute-start | bytes 15368 | tf_op jit(solution)/shard_map/ppermute | solution.py:31
  156.8 31.5 %collective-permute-start.20 = (f32[10,128]{1,0:T(8,128)S(1)}, f32[10,128]{1,0:T(8,128)S(1)}, u32[]{:S(2)}, u32[]{:S(2)}) collective-permute-start(f32[10,128]{1,0:T(8,128)S(1)} %fusion.18.refs_0_), channel_id=1, source_target_pairs={{160,0},{192,32},{224,64},{0,96},{32,128},{64,160},{96,192},{128,2... | collective-permute-start | bytes 15368 | tf_op jit(solution)/shard_map/ppermute | solution.py:31
  183.4 5.8 %collective-permute-start.21 = (f32[10,128]{1,0:T(8,128)S(1)}, f32[10,128]{1,0:T(8,128)S(1)}, u32[]{:S(2)}, u32[]{:S(2)}) collective-permute-start(f32[10,128]{1,0:T(8,128)S(1)} %fusion.18.refs_0_), channel_id=1, source_target_pairs={{192,0},{224,32},{0,64},{32,96},{64,128},{96,160},{128,192},{160,2... | collective-permute-start | bytes 15368 | tf_op jit(solution)/shard_map/ppermute | solution.py:31
  183.4 5.8 %collective-permute-start.22 = (f32[10,128]{1,0:T(8,128)S(1)}, f32[10,128]{1,0:T(8,128)S(1)}, u32[]{:S(2)}, u32[]{:S(2)}) collective-permute-start(f32[10,128]{1,0:T(8,128)S(1)} %fusion.18.refs_0_), channel_id=1, source_target_pairs={{224,0},{0,32},{32,64},{64,96},{96,128},{128,160},{160,192},{192,2... | collective-permute-start | bytes 15368 | tf_op jit(solution)/shard_map/ppermute | solution.py:31
  (14 other events, 184.1 us)
Sparse Core Ops, SparseCore 0:
  21.4 55.5 all-gather.1
where the time goes:
time: 199 us; the launch traced here: 198 us
  starting transfers between devices  71.9 us (36%)
  waiting for transfers between devices  64.5 us (32%)
  Pallas kernels  27.7 us (14%)
  between operations  15 us (8%)
  local copies, waits for them, and re-layouts  13.1 us (7%)
  other arithmetic  3.96 us (2%)
  matrix products  2.15 us (1%)
    ppermute x24, waiting for transfers between devices, ahead(): lax.ppermute(a, axis, tuple((((i + steps) % n, i) for i in range(n))))  51.8 us
    ppermute x24, starting transfers between devices, ahead(): lax.ppermute(a, axis, tuple((((i + steps) % n, i) for i in range(n))))  38.8 us
    all_to_all x4, starting transfers between devices, exchange(): return lax.all_to_all(pieces, axes, split_axis=0, concat_axis=0, tiled=True)  33 us
    pallas_call x1, Pallas kernels, on_device(): pl.pallas_call(forward_kernel, out_shape=(pltpu.HBM((group, 512), f32), p...  15.5 us
    all_to_all x4, waiting for transfers between devices, exchange(): return lax.all_to_all(pieces, axes, split_axis=0, concat_axis=0, tiled=True)  12.7 us
    pallas_call x1, Pallas kernels, on_device(): pl.pallas_call(backward_kernel, out_shape=(VMEM(packed, f32), VMEM(packed...  7.13 us
  transfers between devices with their start and end apart: 29, of which 15 were waited for; matrix products, arithmetic and copies ran while one was open for 6% of the time, Pallas kernels for 0%

commit v1 on v0

--- a/solution.py
+++ b/solution.py
@@ -69,69 +69,85 @@
 
 def forward_kernel(place, *refs):
     a_refs, b_refs = refs[:YS], refs[YS : YS + XS]
-    weights, embed_in, extras = refs[YS + XS : YS + XS + 3]
-    pre_out, states_out, said = refs[YS + XS + 3 : YS + XS + 6]
-    pre, states, embed, held, sems, part_sems, more = refs[YS + XS + 6 :]
-    y, x = place[0], place[1]
-    slot_count = a_refs[0].shape[1]
-    tokens = 2 * slot_count
+    weights, pre, held, sems = refs[YS + XS :]
+    x = place[1]
     heads_width = weights.shape[2]
-
-    def load(xr):
-        return pltpu.make_async_copy(weights.at[lax.rem(x + xr, XS)], held.at[xr], sems.at[xr])
-
-    def parts(xr):
-        found = []
-        for r in range(YS):
-            low = pl.ds(r * tokens, slot_count)
-            high = pl.ds(r * tokens + slot_count, slot_count)
-            for half, (source, to) in enumerate(((a_refs[r].at[xr], low), (b_refs[xr].at[r], high))):
-                found.append(
-                    pltpu.make_async_copy(source, states.at[xr, to], part_sems.at[xr, r, half])
-                )
-        return found
-
-    for xr in range(XS):
-        load(xr).start()
-        for copy in parts(xr):
+    half = pre.shape[0] // 2
+    whole = heads_width // 256
+
+    def loads(n):
+        at = pl.ds(pl.multiple_of(n * 256, 256), 256) if n < whole else pl.ds(n * 256, 128)
+        to = 256 if n < whole else 128
+        return [
+            pltpu.make_async_copy(
+                weights.at[lax.rem(x + xr, XS), :, at], held.at[n, xr, :, :to], sems.at[n, xr]
+            )
+            for xr in range(XS)
+        ]
+
+    for n in range(whole + 1):
+        for copy in loads(n):
             copy.start()
-    fetch = pltpu.make_async_copy(embed_in, embed, more.at[0])
-    fetch.start()
-    keep_states = pltpu.make_async_copy(states, states_out, more.at[1])
-    for xr in range(XS):
-        for copy in parts(xr):
-            copy.wait()
-        if xr == XS - 1:
-            keep_states.start()
-        load(xr).wait()
-
-        def columns(at):
-            part = jnp.dot(states[xr], held[xr, :, at], preferred_element_type=f32)
-            pre[:, at] = part if xr == 0 else pre[:, at] + part
-
-        whole = heads_width // 256
-
-        @pl.loop(0, whole)
-        def _(n):
-            columns(pl.ds(pl.multiple_of(n * 256, 256), 256))
-
-        if heads_width > whole * 256:
-            columns(slice(whole * 256, heads_width))
-
+
+    def columns(n, at, wide):
+        total_a = total_b = None
+        for xr in range(XS):
+            block = held[n, xr, :, :wide]
+            states_a = jnp.concatenate([a_refs[r][xr] for r in range(YS)], axis=0)
+            states_b = b_refs[xr][...].reshape(half, states_a.shape[1])
+            part_a = jnp.dot(states_a, block, preferred_element_type=f32)
+            part_b = jnp.dot(states_b, block, preferred_element_type=f32)
+            total_a = part_a if xr == 0 else total_a + part_a
+            total_b = part_b if xr == 0 else total_b + part_b
+        pre[:half, at] = total_a
+        pre[half:, at] = total_b
+
+    @pl.loop(0, whole)
+    def _(n):
+        for xr in range(XS):
+            pltpu.make_async_copy(
+                weights.at[xr, :, :256], held.at[n, xr], sems.at[n, xr]
+            ).wait()
+        columns(n, pl.ds(pl.multiple_of(n * 256, 256), 256), 256)
+
+    for copy in loads(whole):
+        copy.wait()
+    columns(whole, slice(whole * 256, heads_width), heads_width - whole * 256)
+
+
+def score_kernel(place, pre, back, extras, said, kept, embed):
+    y = place[0]
+    heads_width = pre.shape[1]
     cols = heads_width // 4
-    keep_pre = pltpu.make_async_copy(pre.at[:, : pre_out.shape[1]], pre_out, more.at[2])
-    keep_pre.start()
-    fetch.wait()
+    group = pre.shape[0]
+    slot_count = group // (2 * YS)
+    slots = lax.broadcasted_iota(jnp.int32, (group, 1), 0)
+    source = lax.rem(lax.rem(lax.div(slots, 2), YS) + YS - y, YS)
+    spot = back[:, cols : cols + 1].astype(f32).astype(jnp.int32)
+    late = (spot >= slot_count).astype(jnp.int32)
+    token = late * (group // 2) + source * slot_count + spot - late * slot_count
+    one_hot = token == lax.broadcasted_iota(jnp.int32, (group, group), 1)
+    rows = lax.dot_general(
+        one_hot.astype(f32).astype(bf16),
+        back[:, :cols],
+        (((0,), (0,)), ((), ())),
+        preferred_element_type=f32,
+    ).astype(bf16)
+    for h in range(4):
+        embed[:, h * cols : (h + 1) * cols] = rows
+    kept[...] = embed[:, : kept.shape[1]]
 
     @pl.loop(0, YS)
     def _(r):
-        rows = pl.ds(pl.multiple_of(r * tokens, tokens), tokens)
         total = extras[...]
+        low = pl.ds(pl.multiple_of(r * slot_count, slot_count), slot_count)
+        high = pl.ds(pl.multiple_of(group // 2 + r * slot_count, slot_count), slot_count)
         for n in range(heads_width // 128):
             lanes = slice(n * 128, (n + 1) * 128)
-            p = pre[rows, lanes]
+            p = jnp.concatenate([pre[low, lanes], pre[high, lanes]], axis=0)
+            e = jnp.concatenate([embed[low, lanes], embed[high, lanes]], axis=0)
             g = 0.5 * p * (1.0 + jnp.tanh(root * (p + cubic * (p * p * p))))
-            g = g * embed[rows, lanes].astype(f32)
+            g = g * e.astype(f32)
             lane = lax.broadcasted_iota(jnp.int32, (8, 128), 1) + n * 128
             head = lax.broadcasted_iota(jnp.int32, (8, 128), 0)
             chosen = ((lane >= head * cols) & (lane < (head + 1) * cols)).astype(f32).astype(bf16)
@@ -142,39 +158,23 @@
         for copy in range(YS * XS):
             said[copy, lax.rem(y + r, YS)] = total
 
-    keep_states.wait()
-    keep_pre.wait()
-
-
-def backward_kernel(
-    place, bias, said, pre_in, embed_in, states_in, keep, send, small, value, *scratch
-):
-    pre, embed, states, held, grads, sems, more = scratch
-
-    def load(xr):
-        return pltpu.make_async_copy(states_in.at[xr], states.at[xr], sems.at[xr])
-
-    fetch_pre = pltpu.make_async_copy(pre_in, pre, more.at[0])
-    fetch_embed = pltpu.make_async_copy(embed_in.at[:, : embed.shape[1]], embed, more.at[1])
-    fetch_pre.start()
-    fetch_embed.start()
-    for xr in range(XS):
-        load(xr).start()
+
+def backward_kernel(place, bias, said, pre, embed, *refs):
+    a_refs, b_refs = refs[:YS], refs[YS : YS + XS]
+    keep, send, small, value, held, grads = refs[YS + XS :]
     y, x, core = place[0], place[1], place[2]
     tokens = said.shape[4]
-    width = states.shape[2]
+    slot_count = tokens // 2
+    half = YS * slot_count
+    width = a_refs[0].shape[2]
     share = width // (ZS // XS * YS * CS)
     cols = width // YS
     both = 2 * cols
     slot = lax.rem(lax.broadcasted_iota(jnp.int32, (1, tokens), 1), tokens // 2).astype(f32)
     row = lax.broadcasted_iota(jnp.int32, (8, tokens), 0)
     value[...] = jnp.zeros_like(value)
-    fetch_pre.wait()
-    fetch_embed.wait()
-    load(0).wait()
-
-    def prompts(r, sums):
-        bias_sum, loss_sum, count_sum = sums
+    bias_sum = loss_sum = count_sum = jnp.zeros((1, tokens), f32)
+    for r in range(YS):
         ya = lax.rem(y + r, YS)
         scores = said[0, 0, ya]
         for i in range(1, YS * XS):
@@ -205,43 +205,40 @@
         third = e - first - second
         thirds = jnp.where(row == 0, first, jnp.where(row == 1, second, third))
         thirds = jnp.where(row < 3, thirds, 0.0).astype(bf16)
-        rows = pl.ds(pl.multiple_of(r * tokens, tokens), tokens)
-        value[...] = value[...] + jnp.dot(thirds, states[0, rows], preferred_element_type=f32)
+        value[...] = (
+            value[...]
+            + jnp.dot(thirds[:, :slot_count], a_refs[r][0], preferred_element_type=f32)
+            + jnp.dot(thirds[:, slot_count:], b_refs[0][r], preferred_element_type=f32)
+        )
         upright = jnp.transpose(jnp.where(row == 0, g_one, jnp.where(row == 1, g_two, 0.0)))
-        left, right = upright[:, 0:1], upright[:, 1:2]
-        for n in range(held.shape[1] // 128):
-            lanes = slice(n * 128, (n + 1) * 128)
-            lane = lax.broadcasted_iota(jnp.int32, (tokens, 128), 1) + n * 128
-            g = jnp.where(lane < cols, left, jnp.where(lane < both, right, 0.0))
-            p = pre[rows, lanes]
-            t = jnp.tanh(root * (p + cubic * (p * p * p)))
-            steep = 0.5 * (1.0 + t) + 0.5 * p * (1.0 - t * t) * (
-                root * (1.0 + 3.0 * cubic * (p * p))
-            )
-            held[rows, lanes] = (g * embed[rows, lanes].astype(f32) * steep).astype(bf16)
-        return bias_sum, loss_sum, count_sum
-
-    nothing = jnp.zeros((1, tokens), f32)
-    bias_sum, loss_sum, count_sum = lax.fori_loop(0, YS, prompts, (nothing, nothing, nothing))
+        for part in range(2):
+            left = upright[part * slot_count : (part + 1) * slot_count, 0:1]
+            right = upright[part * slot_count : (part + 1) * slot_count, 1:2]
+            at = part * half + r * slot_count
+            rows = slice(at, at + slot_count)
+            for n in range(held.shape[1] // 128):
+                lanes = slice(n * 128, (n + 1) * 128)
+                lane = lax.broadcasted_iota(jnp.int32, (slot_count, 128), 1) + n * 128
+                g = jnp.where(lane < cols, left, jnp.where(lane < both, right, 0.0))
+                p = pre[rows, lanes]
+                t = jnp.tanh(root * (p + cubic * (p * p * p)))
+                steep = 0.5 * (1.0 + t) + 0.5 * p * (1.0 - t * t) * (
+                    root * (1.0 + 3.0 * cubic * (p * p))
+                )
+                held[rows, lanes] = (g * embed[rows, lanes].astype(f32) * steep).astype(bf16)
     small[...] = jnp.where(
         row == 0, bias_sum, jnp.where(row == 1, loss_sum, jnp.where(row == 2, count_sum, 0.0))
     )
 
-    @pl.loop(0, XS)
-    def _(xr):
+    def against(xr, states_b):
+        states_a = jnp.concatenate([ref[xr] for ref in a_refs], axis=0)
         xa = lax.rem(x + xr, XS)
-
-        @pl.when(xr > 0)
-        def _():
-            load(xr).wait()
-
         for n in range(held.shape[1] // 256):
             lanes = slice(n * 256, (n + 1) * 256)
             grads[:, lanes] = lax.dot_general(
-                states[xr],
-                held[:, lanes],
-                (((0,), (0,)), ((), ())),
-                preferred_element_type=f32,
+                states_a, held[:half, lanes], (((0,), (0,)), ((), ())), preferred_element_type=f32
+            ) + lax.dot_general(
+                states_b, held[half:, lanes], (((0,), (0,)), ((), ())), preferred_element_type=f32
             )
         for z2 in range(ZS // XS):
             for yy in range(YS):
@@ -263,6 +260,9 @@
                 send[to, yy, rows] = jnp.concatenate(
                     [theirs[:32], theirs[share - 32 :]], axis=1
                 ).astype(bf16)
+
+    for xr in range(XS):
+        against(xr, b_refs[xr][...].reshape(half, width))
 
 
 def finish_kernel(*refs):
@@ -291,7 +291,7 @@
         two[:, y * cols : (y + 1) * cols] = row[:, cols:]
 
 
-def lookup(ids, table, y):
+def lookup(ids, table):
     count = ids.shape[0]
     local_rows = table.shape[0]
     holders = lax.axis_size(ROWS)
@@ -314,18 +314,7 @@
     )
     sent = jnp.concatenate([found, where], axis=-1).reshape(holders, YS * per_holder, columns + 1)
     back = exchange(sent, ROWS)
-    back = back.reshape(holders * YS * per_holder, columns + 1)
-    slots = jnp.arange(holders * YS * per_holder, dtype=jnp.int32)
-    source = (slots // per_holder % YS + YS - y) % YS
-    token = source * count + back[:, columns].astype(jnp.int32)
-    one_hot = (token[:, None] == jnp.arange(YS * count, dtype=jnp.int32)[None, :]).astype(bf16)
-    rows = back[:, :columns]
-    return lax.dot_general(
-        one_hot,
-        jnp.concatenate([rows, rows, rows, rows], axis=1),
-        (((0,), (0,)), ((), ())),
-        preferred_element_type=f32,
-    ).astype(bf16)
+    return back.reshape(holders * YS * per_holder, columns + 1)
 
 
 def on_device(
@@ -368,7 +357,7 @@
     b_part = jnp.stack([half_b] + b_steps)
     a_parts = [a_part] + [ahead(a_part, "y", s) for s in range(1, YS)]
     b_parts = [b_part] + [ahead(b_part, "x", s) for s in range(1, XS)]
-    embed = lookup(actions.reshape(tokens), table, y)
+    back = lookup(actions.reshape(tokens), table)
 
     value_part = jnp.dot(
         hidden.reshape(tokens, width), value_weight, preferred_element_type=f32
@@ -383,29 +372,31 @@
         ]
     )
     group = YS * tokens
-    pre, states, said = pl.pallas_call(
+    pre = pl.pallas_call(
         forward_kernel,
-        out_shape=(
-            pltpu.HBM((group, 512), f32),
-            pltpu.HBM((XS, group, width), bf16),
-            jax.ShapeDtypeStruct((YS * XS, YS, 8, tokens), f32),
-        ),
-        in_specs=[smem] + [vmem] * (YS + XS) + [anywhere, anywhere, vmem],
-        out_specs=(anywhere, anywhere, vmem),
+        out_shape=jax.ShapeDtypeStruct((group, 4 * cols), f32),
+        in_specs=[smem] + [vmem] * (YS + XS) + [anywhere],
+        out_specs=vmem,
         scratch_shapes=[
-            VMEM((group, 4 * cols), f32),
-            VMEM((XS, group, width), bf16),
-            VMEM((group, 4 * cols), bf16),
-            VMEM((XS, width, 4 * cols), bf16),
-            pltpu.SemaphoreType.DMA((XS,)),
-            pltpu.SemaphoreType.DMA((XS, YS, 2)),
-            pltpu.SemaphoreType.DMA((3,)),
+            VMEM((4 * cols // 256 + 1, XS, width, 256), bf16),
+            pltpu.SemaphoreType.DMA((4 * cols // 256 + 1, XS)),
         ],
         compiler_params=limit,
         cost_estimate=pl.CostEstimate(
             flops=2 * group * XS * width * 4 * cols, bytes_accessed=12 << 20, transcendentals=0
         ),
-    )(place, *map(near, a_parts), *map(near, b_parts), far(weights), far(embed), extras)
+    )(place, *a_parts, *b_parts, far(weights))
+    said, embed = pl.pallas_call(
+        score_kernel,
+        out_shape=(
+            jax.ShapeDtypeStruct((YS * XS, YS, 8, tokens), f32),
+            jax.ShapeDtypeStruct((group, 512), bf16),
+        ),
+        in_specs=[smem] + [vmem] * 3,
+        out_specs=(vmem, vmem),
+        scratch_shapes=[VMEM((group, 4 * cols), bf16)],
+        compiler_params=limit,
+    )(place, pre, back, extras)
 
     said = exchange(said, ("y", "x")).reshape(YS, XS, YS, 8, tokens)
     packed = (ZS, YS, 3 * share + 32, 128)
@@ -417,22 +408,14 @@
             jax.ShapeDtypeStruct((8, tokens), f32),
             jax.ShapeDtypeStruct((8, width), f32),
         ),
-        in_specs=[smem, smem, vmem] + [anywhere] * 3,
+        in_specs=[smem, smem] + [vmem] * (3 + YS + XS),
         out_specs=(vmem, vmem, vmem, vmem),
-        scratch_shapes=[
-            VMEM((group, 512), f32),
-            VMEM((group, 512), bf16),
-            VMEM((XS, group, width), bf16),
-            VMEM((group, 512), bf16),
-            VMEM((width, 512), f32),
-            pltpu.SemaphoreType.DMA((XS,)),
-            pltpu.SemaphoreType.DMA((2,)),
-        ],
+        scratch_shapes=[VMEM((group, 512), bf16), VMEM((width, 512), f32)],
         compiler_params=limit,
         cost_estimate=pl.CostEstimate(
             flops=2 * group * XS * width * 512, bytes_accessed=12 << 20, transcendentals=0
         ),
-    )(place, value_bias, near(said), far(pre), far(embed), far(states))
+    )(place, value_bias, near(said), pre, embed, *a_parts, *b_parts)
     terms = (keep + ahead(send, "c", 1).astype(f32)).astype(bf16)
     landed = exchange(terms.reshape(ZS * YS, *packed[2:]), ("z", "y")).reshape(packed)
 

time: 199 us -> 202 us (1.015)
  waiting for transfers between devices: 64.5 us -> 49.7 us
  local copies, waits for them, and re-layouts: 13.1 us -> 27.5 us
  Pallas kernels: 27.7 us -> 20.8 us
  starting transfers between devices: 71.9 us -> 77.4 us
  other arithmetic: 3.96 us -> 8.59 us
    unnamed x36 -> x49, local copies, waits for them, and re-layouts: 3.54 us -> 15.6 us
    ppermute x24, waiting for transfers between devices: 51.8 us -> 43.3 us  [ahead(): lax.ppermute(a, axis, tuple((((i + steps) % n, i) for i in range(n))))]
    all_to_all x4, starting transfers between devices: 33 us -> 39.3 us  [exchange(): return lax.all_to_all(pieces, axes, split_axis=0, concat_axis=0, tiled=True)]
    all_to_all x4, waiting for transfers between devices: 12.7 us -> 6.44 us  [exchange(): return lax.all_to_all(pieces, axes, split_axis=0, concat_axis=0, tiled=True)]
    pallas_call x1 -> x2, Pallas kernels: 15.5 us -> 11.6 us  [the longest x1 7.5 us: on_device(): pl.pallas_call(forward_kernel, out_shape=jax.ShapeDtypeStruct((group, 4 *...]
    pallas_call x1, Pallas kernels: 7.13 us -> 4.01 us  [on_device(): pl.pallas_call(backward_kernel, out_shape=(VMEM(packed, f32), VMEM(packed...]
  transfers between devices with their start and end apart: 29 -> 29, of which waited for: 15 -> 9; matrix products, arithmetic and copies ran while one was open for 6% -> 9% of each run, Pallas kernels for 0% -> 4%
where the time goes in v1:
time: 202 us; the launch traced here: 200 us
  starting transfers between devices  77.4 us (38%)
  waiting for transfers between devices  49.7 us (25%)
  local copies, waits for them, and re-layouts  27.5 us (14%)
  Pallas kernels  20.8 us (10%)
  between operations  14.9 us (7%)
  other arithmetic  8.59 us (4%)
    ppermute x24, waiting for transfers between devices, ahead(): lax.ppermute(a, axis, tuple((((i + steps) % n, i) for i in range(n))))  43.3 us
    all_to_all x4, starting transfers between devices, exchange(): return lax.all_to_all(pieces, axes, split_axis=0, concat_axis=0, tiled=True)  39.3 us
    ppermute x24, starting transfers between devices, ahead(): lax.ppermute(a, axis, tuple((((i + steps) % n, i) for i in range(n))))  38.1 us
    unnamed x49, local copies, waits for them, and re-layouts  15.6 us
    pallas_call x1, Pallas kernels, on_device(): pl.pallas_call(forward_kernel, out_shape=jax.ShapeDtypeStruct((group, 4 *...  7.5 us
    all_to_all x4, waiting for transfers between devices, exchange(): return lax.all_to_all(pieces, axes, split_axis=0, concat_axis=0, tiled=True)  6.44 us
    pallas_call x1, Pallas kernels, on_device(): pl.pallas_call(score_kernel, out_shape=(jax.ShapeDtypeStruct((YS * XS, YS...  4.13 us
  transfers between devices with their start and end apart: 29, of which 9 were waited for; matrix products, arithmetic and copies ran while one was open for 9% of the time, Pallas kernels for 4%

profile of v1, /device:TPU:8, one launch (start us, length us, event | category | flops | bytes accessed | tf_op | source)
XLA Modules:
  0.0 200.0 jit_solution(16700447821035694828)
XLA Ops:
  7.9 2.2 %shard_map.162 = (bf16[56,896]{1,0:T(8,128)(2,1)}, bf16[56,896]{1,0:T(8,128)(2,1)}, bf16[56,896]{1,0:T(8,128)(2,1)}, bf16[56,896]{1,0:T(8,128)(2,1)}, bf16[64,896]{1,0:T(8,128)(2,1)}, /*index=5*/bf16[64,896]{1,0:T(8,128)(2,1)}) custom-call(s32[3]{0:T(128)} %pad_add_fusion.place, bf16[56,896]{1,0:T(8,128)(2,1)} %one.1, bf16[56,896]{1,0:T(8,128)(2,1)} %two.1, ...), custom_call_target="tpu_custom_call" | custom-call | tf_op jit(solution)/shard_map/pallas_call | solution.py:338
  10.1 2.2 %collective-permute-start.12 = (bf16[56,896]{1,0:T(8,128)(2,1)}, bf16[56,896]{1,0:T(8,128)(2,1)S(1)}, u32[]{:S(2)}, u32[]{:S(2)}) collective-permute-start(bf16[56,896]{1,0:T(8,128)(2,1)} %get-tuple-element.26), channel_id=1, source_target_pairs={{8,0},{16,8},{24,16},{0,24},{9,1},{17,9},{25,17},{1,25},{10,2},{18... | collective-permute-start | bytes 301064 | tf_op jit(solution)/shard_map/ppermute | solution.py:31
  13.2 1.9 collective-permute-start.14
  15.3 3.3 %collective-permute-done.13.refs_2_ = bf16[56,896]{1,0:T(8,128)(2,1)S(1)} collective-permute-done((bf16[56,896]{1,0:T(8,128)(2,1)}, bf16[56,896]{1,0:T(8,128)(2,1)S(1)}, u32[]{:S(2)}, u32[]{:S(2)}) %collective-permute-start.13) | collective-permute-done | bytes 100384 | tf_op jit(solution)/shard_map/ppermute | solution.py:31
  19.5 1.8 shard_map.163
  24.1 12.0 %all-to-all-start = ((s32[64,1,2]{2,1,0:T(1,128)}), s32[64,1,2]{2,1,0:T(1,128)S(1)}, u32[]{:S(2)}, u32[]{:S(2)}) async-start(s32[64,1,2]{2,1,0:T(1,128)} %bitcast.13), calls=%async_computation | async-start | bytes 65536 | tf_op jit(solution)/shard_map/all_to_all | solution.py:26
  36.1 1.5 collective-permute-start.8
  38.2 2.1 %collective-permute-start.7 = (bf16[64,896]{1,0:T(8,128)(2,1)}, bf16[64,896]{1,0:T(8,128)(2,1)S(1)}, u32[]{:S(2)}, u32[]{:S(2)}) collective-permute-start(bf16[64,896]{1,0:T(8,128)(2,1)} %get-tuple-element.24), channel_id=1, source_target_pairs={{16,0},{24,8},{0,16},{8,24},{17,1},{25,9},{1,17},{9,25},{18,2},{26... | collective-permute-start | bytes 344072 | tf_op jit(solution)/shard_map/ppermute | solution.py:31
  40.3 2.8 %collective-permute-start = (bf16[64,896]{1,0:T(8,128)(2,1)}, bf16[64,896]{1,0:T(8,128)(2,1)S(1)}, u32[]{:S(2)}, u32[]{:S(2)}) collective-permute-start(bf16[64,896]{1,0:T(8,128)(2,1)} %get-tuple-element.23), channel_id=1, source_target_pairs={{1,0},{2,1},{3,2},{0,3},{5,4},{6,5},{7,6},{4,7},{9,8},{10,9},{11,1... | collective-permute-start | bytes 344072 | tf_op jit(solution)/shard_map/ppermute | solution.py:31
  48.1 2.1 %collective-permute-start.10 = (bf16[4,64,896]{2,1,0:T(8,128)(2,1)S(1)}, bf16[4,64,896]{2,1,0:T(8,128)(2,1)S(1)}, u32[]{:S(2)}, u32[]{:S(2)}) collective-permute-start(bf16[4,64,896]{2,1,0:T(8,128)(2,1)S(1)} %pad_maximum_fusion.1.refs_4_), channel_id=1, source_target_pairs={{2,0},{3,1},{0,2},{1,3},{6,4},{7,5},{4,6},{5,7},{10,8},{11,9},{8,1... | collective-permute-start | bytes 1376264 | tf_op jit(solution)/shard_map/ppermute | solution.py:31
  51.8 2.1 %collective-permute-start.9 = (bf16[4,64,896]{2,1,0:T(8,128)(2,1)S(1)}, bf16[4,64,896]{2,1,0:T(8,128)(2,1)S(1)}, u32[]{:S(2)}, u32[]{:S(2)}) collective-permute-start(bf16[4,64,896]{2,1,0:T(8,128)(2,1)S(1)} %pad_maximum_fusion.1.refs_4_), channel_id=1, source_target_pairs={{1,0},{2,1},{3,2},{0,3},{5,4},{6,5},{7,6},{4,7},{9,8},{10,9},{11,1... | collective-permute-start | bytes 1376264 | tf_op jit(solution)/shard_map/ppermute | solution.py:31
  53.9 7.5 %collective-permute-done.2 = bf16[64,896]{1,0:T(8,128)(2,1)S(1)} collective-permute-done((bf16[64,896]{1,0:T(8,128)(2,1)}, bf16[64,896]{1,0:T(8,128)(2,1)S(1)}, u32[]{:S(2)}, u32[]{:S(2)}) %collective-permute-start.2) | collective-permute-done | bytes 114720 | tf_op jit(solution)/shard_map/ppermute | solution.py:31
  62.4 1.5 collective-permute-start.3
  65.1 1.6 collective-permute-start.5
  66.7 3.8 %gather_fusion = bf16[128,896]{1,0:T(8,128)(2,1)S(1)} fusion(bf16[2376,896]{1,0:T(8,128)(2,1)} %param.15, s32[1024]{0:T(1024)S(1)} %pad_clamp_fusion), kind=kCustom, calls=%fused_computation | custom fusion | bytes 459264 | tf_op jit(solution)/shard_map/gather | solution.py:308
  74.3 1.9 reshape.176
  76.2 10.8 %all-to-all-start.1 = ((bf16[64,8,225]{2,1,0:T(8,128)(2,1)}), bf16[64,8,225]{2,1,0:T(8,128)(2,1)S(1)}, u32[]{:S(2)}, u32[]{:S(2)}) async-start(bf16[64,8,225]{2,1,0:T(8,128)(2,1)} %reshape.176), calls=%async_computation.1 | async-start | bytes 524288 | tf_op jit(solution)/shard_map/all_to_all | solution.py:26
  95.5 7.5 %shard_map.164.pre = f32[512,896]{1,0:T(8,128)S(1)} custom-call(s32[3]{0:T(128)S(1)} %copy-done, bf16[4,64,896]{2,1,0:T(8,128)(2,1)S(1)} %pad_maximum_fusion.refs_0_, bf16[4,64,896]{2,1,0:T(8,128)(2,1)S(1)} %copy-done.12, bf16[4,64,896]{2,1,0:T(8,128)(2,1)S(1)} %copy-done.15, bf16[4,64,896]{2,1,0:T(8,128)(2,1)} %collective-permute-done.5.refs_3_, ...), custom_call_target="tpu_custom_call" | custom-call | flops 3288334336 | bytes 12582912 | tf_op jit(solution)/shard_map/pallas_call | solution.py:375
  103.0 4.1 %shard_map.165 = (f32[16,4,8,128]{3,2,1,0:T(8,128)}, bf16[512,512]{1,0:T(8,128)(2,1)S(1)}) custom-call(s32[3]{0:T(128)S(1)} %copy-done, f32[512,896]{1,0:T(8,128)S(1)} %shard_map.164.pre, bf16[512,225]{1,0:T(8,128)(2,1)S(1)} %bitcast.41, f32[8,128]{1,0:T(8,128)S(1)} %concatenate.10.extras), custom_call_target="tpu_custom_call" | custom-call | tf_op jit(solution)/shard_map/pallas_call | solution.py:389
  107.9 7.1 %all-to-all-start.2 = ((f32[16,4,8,128]{3,2,1,0:T(8,128)}), f32[16,4,8,128]{3,2,1,0:T(8,128)S(1)}, u32[]{:S(2)}, u32[]{:S(2)}) async-start(f32[16,4,8,128]{3,2,1,0:T(8,128)} %get-tuple-element.29), calls=%async_computation.2 | async-start | bytes 524288 | tf_op jit(solution)/shard_map/all_to_all | solution.py:26
  115.7 6.4 %all-to-all-done.2 = f32[16,4,8,128]{3,2,1,0:T(8,128)S(1)} async-done(((f32[16,4,8,128]{3,2,1,0:T(8,128)}), f32[16,4,8,128]{3,2,1,0:T(8,128)S(1)}, u32[]{:S(2)}, u32[]{:S(2)}) %all-to-all-start.2) | async-done | bytes 262176 | tf_op jit(solution)/shard_map/all_to_all | solution.py:26
  128.3 4.0 %shard_map.166 = (f32[8,4,200,128]{3,2,1,0:T(8,128)S(1)}, bf16[8,4,200,128]{3,2,1,0:T(8,128)(2,1)S(1)}, f32[8,128]{1,0:T(8,128)S(1)}, f32[8,896]{1,0:T(8,128)S(1)}) custom-call(s32[3]{0:T(128)S(1)} %copy-done, f32[1]{0:T(128)S(6)} %copy.51.bias, f32[4,4,4,8,128]{4,3,2,1,0:T(8,128)S(1)} %bitcast.42, f32[512,896]{1,0:T(8,128)S(1)} %shard_map.164.pre, ...), custom_call_target="tpu_custom_call" | custom-call | flops 1879048192 | bytes 12582912 | tf_op jit(solution)/shard_map/pallas_call | solution.py:403
  132.4 3.5 %collective-permute-done.23 = bf16[8,4,200,128]{3,2,1,0:T(8,128)(2,1)S(1)} collective-permute-done((bf16[8,4,200,128]{3,2,1,0:T(8,128)(2,1)S(1)}, bf16[8,4,200,128]{3,2,1,0:T(8,128)(2,1)S(1)}, u32[]{:S(2)}, u32[]{:S(2)}) %collective-permute-start.23) | collective-permute-done | bytes 1638432 | tf_op jit(solution)/shard_map/ppermute | solution.py:31
  135.9 1.6 add_convert_fusion
  137.5 9.4 %all-to-all-start.3 = ((bf16[32,200,128]{2,1,0:T(8,128)(2,1)}), bf16[32,200,128]{2,1,0:T(8,128)(2,1)S(1)}, u32[]{:S(2)}, u32[]{:S(2)}) async-start(bf16[32,200,128]{2,1,0:T(8,128)(2,1)} %bitcast.25), calls=%async_computation.3 | async-start | bytes 3276800 | tf_op jit(solution)/shard_map/all_to_all | solution.py:26
  148.3 2.8 %collective-permute-start.16 = (f32[10,128]{1,0:T(8,128)S(1)}, f32[10,128]{1,0:T(8,128)S(1)}, u32[]{:S(2)}, u32[]{:S(2)}) collective-permute-start(f32[10,128]{1,0:T(8,128)S(1)} %fusion.3.refs_0_), channel_id=1, source_target_pairs={{32,0},{64,32},{96,64},{128,96},{160,128},{192,160},{224,192},{0,2... | collective-permute-start | bytes 15368 | tf_op jit(solution)/shard_map/ppermute | solution.py:31
  151.1 2.3 %collective-permute-start.17 = (f32[10,128]{1,0:T(8,128)S(1)}, f32[10,128]{1,0:T(8,128)S(1)}, u32[]{:S(2)}, u32[]{:S(2)}) collective-permute-start(f32[10,128]{1,0:T(8,128)S(1)} %fusion.3.refs_0_), channel_id=1, source_target_pairs={{64,0},{96,32},{128,64},{160,96},{192,128},{224,160},{0,192},{32,2... | collective-permute-start | bytes 15368 | tf_op jit(solution)/shard_map/ppermute | solution.py:31
  153.4 1.4 collective-permute-start.18
  154.8 3.7 %collective-permute-start.19 = (f32[10,128]{1,0:T(8,128)S(1)}, f32[10,128]{1,0:T(8,128)S(1)}, u32[]{:S(2)}, u32[]{:S(2)}) collective-permute-start(f32[10,128]{1,0:T(8,128)S(1)} %fusion.3.refs_0_), channel_id=1, source_target_pairs={{128,0},{160,32},{192,64},{224,96},{0,128},{32,160},{64,192},{96,2... | collective-permute-start | bytes 15368 | tf_op jit(solution)/shard_map/ppermute | solution.py:31
  158.7 26.4 %collective-permute-done.16.refs_1_ = f32[10,128]{1,0:T(8,128)S(1)} collective-permute-done((f32[10,128]{1,0:T(8,128)S(1)}, f32[10,128]{1,0:T(8,128)S(1)}, u32[]{:S(2)}, u32[]{:S(2)}) %collective-permute-start.16) | collective-permute-done | bytes 5152 | tf_op jit(solution)/shard_map/ppermute | solution.py:31
  185.1 4.2 %collective-permute-start.22 = (f32[10,128]{1,0:T(8,128)S(1)}, f32[10,128]{1,0:T(8,128)S(1)}, u32[]{:S(2)}, u32[]{:S(2)}) collective-permute-start(f32[10,128]{1,0:T(8,128)S(1)} %fusion.3.refs_0_), channel_id=1, source_target_pairs={{224,0},{0,32},{32,64},{64,96},{96,128},{128,160},{160,192},{192,2... | collective-permute-start | bytes 15368 | tf_op jit(solution)/shard_map/ppermute | solution.py:31
  191.9 1.2 fusion.4
  (127 shorter events, 38.1 us)
Async XLA Ops:
  7.2 84.2 %all-gather.2.cloned.1.call-start = ((), (), s32[]{:S(2)}) async-start(), calls=%async_computation.4 | async-start | bytes 6823936 | tf_op jit(solution)/shard_map/all_gather | solution.py:352
  10.1 5.2 %collective-permute-start.12 = (bf16[56,896]{1,0:T(8,128)(2,1)}, bf16[56,896]{1,0:T(8,128)(2,1)S(1)}, u32[]{:S(2)}, u32[]{:S(2)}) collective-permute-start(bf16[56,896]{1,0:T(8,128)(2,1)} %get-tuple-element.26), channel_id=1, source_target_pairs={{8,0},{16,8},{24,16},{0,24},{9,1},{17,9},{25,17},{1,25},{10,2},{18... | collective-permute-start | bytes 301064 | tf_op jit(solution)/shard_map/ppermute | solution.py:31
  12.3 6.4 %collective-permute-start.13 = (bf16[56,896]{1,0:T(8,128)(2,1)}, bf16[56,896]{1,0:T(8,128)(2,1)S(1)}, u32[]{:S(2)}, u32[]{:S(2)}) collective-permute-start(bf16[56,896]{1,0:T(8,128)(2,1)} %get-tuple-element.27), channel_id=1, source_target_pairs={{16,0},{24,8},{0,16},{8,24},{17,1},{25,9},{1,17},{9,25},{18,2},{26... | collective-permute-start | bytes 301064 | tf_op jit(solution)/shard_map/ppermute | solution.py:31
  13.2 5.7 %collective-permute-start.14 = (bf16[56,896]{1,0:T(8,128)(2,1)}, bf16[56,896]{1,0:T(8,128)(2,1)S(1)}, u32[]{:S(2)}, u32[]{:S(2)}) collective-permute-start(bf16[56,896]{1,0:T(8,128)(2,1)} %get-tuple-element.28), channel_id=1, source_target_pairs={{24,0},{0,8},{8,16},{16,24},{25,1},{1,9},{9,17},{17,25},{26,2},{2,... | collective-permute-start | bytes 301064 | tf_op jit(solution)/shard_map/ppermute | solution.py:31
  24.1 22.0 %all-to-all-start = ((s32[64,1,2]{2,1,0:T(1,128)}), s32[64,1,2]{2,1,0:T(1,128)S(1)}, u32[]{:S(2)}, u32[]{:S(2)}) async-start(s32[64,1,2]{2,1,0:T(1,128)} %bitcast.13), calls=%async_computation | async-start | bytes 65536 | tf_op jit(solution)/shard_map/all_to_all | solution.py:26
  36.1 10.1 %collective-permute-start.8 = (bf16[64,896]{1,0:T(8,128)(2,1)}, bf16[64,896]{1,0:T(8,128)(2,1)S(1)}, u32[]{:S(2)}, u32[]{:S(2)}) collective-permute-start(bf16[64,896]{1,0:T(8,128)(2,1)} %get-tuple-element.24), channel_id=1, source_target_pairs={{24,0},{0,8},{8,16},{16,24},{25,1},{1,9},{9,17},{17,25},{26,2},{2,... | collective-permute-start | bytes 344072 | tf_op jit(solution)/shard_map/ppermute | solution.py:31
  37.6 9.5 %collective-permute-start.6 = (bf16[64,896]{1,0:T(8,128)(2,1)}, bf16[64,896]{1,0:T(8,128)(2,1)S(1)}, u32[]{:S(2)}, u32[]{:S(2)}) collective-permute-start(bf16[64,896]{1,0:T(8,128)(2,1)} %get-tuple-element.24), channel_id=1, source_target_pairs={{8,0},{16,8},{24,16},{0,24},{9,1},{17,9},{25,17},{1,25},{10,2},{18... | collective-permute-start | bytes 344072 | tf_op jit(solution)/shard_map/ppermute | solution.py:31
  38.2 9.0 %collective-permute-start.7 = (bf16[64,896]{1,0:T(8,128)(2,1)}, bf16[64,896]{1,0:T(8,128)(2,1)S(1)}, u32[]{:S(2)}, u32[]{:S(2)}) collective-permute-start(bf16[64,896]{1,0:T(8,128)(2,1)} %get-tuple-element.24), channel_id=1, source_target_pairs={{16,0},{24,8},{0,16},{8,24},{17,1},{25,9},{1,17},{9,25},{18,2},{26... | collective-permute-start | bytes 344072 | tf_op jit(solution)/shard_map/ppermute | solution.py:31
  40.3 11.5 %collective-permute-start = (bf16[64,896]{1,0:T(8,128)(2,1)}, bf16[64,896]{1,0:T(8,128)(2,1)S(1)}, u32[]{:S(2)}, u32[]{:S(2)}) collective-permute-start(bf16[64,896]{1,0:T(8,128)(2,1)} %get-tuple-element.23), channel_id=1, source_target_pairs={{1,0},{2,1},{3,2},{0,3},{5,4},{6,5},{7,6},{4,7},{9,8},{10,9},{11,1... | collective-permute-start | bytes 344072 | tf_op jit(solution)/shard_map/ppermute | solution.py:31
  43.0 10.8 %collective-permute-start.1 = (bf16[64,896]{1,0:T(8,128)(2,1)}, bf16[64,896]{1,0:T(8,128)(2,1)S(1)}, u32[]{:S(2)}, u32[]{:S(2)}) collective-permute-start(bf16[64,896]{1,0:T(8,128)(2,1)} %get-tuple-element.23), channel_id=1, source_target_pairs={{2,0},{3,1},{0,2},{1,3},{6,4},{7,5},{4,6},{5,7},{10,8},{11,9},{8,1... | collective-permute-start | bytes 344072 | tf_op jit(solution)/shard_map/ppermute | solution.py:31
  46.2 15.2 %collective-permute-start.2 = (bf16[64,896]{1,0:T(8,128)(2,1)}, bf16[64,896]{1,0:T(8,128)(2,1)S(1)}, u32[]{:S(2)}, u32[]{:S(2)}) collective-permute-start(bf16[64,896]{1,0:T(8,128)(2,1)} %get-tuple-element.23), channel_id=1, source_target_pairs={{3,0},{0,1},{1,2},{2,3},{7,4},{4,5},{5,6},{6,7},{11,8},{8,9},{9,10... | collective-permute-start | bytes 344072 | tf_op jit(solution)/shard_map/ppermute | solution.py:31
  48.1 17.0 %collective-permute-start.10 = (bf16[4,64,896]{2,1,0:T(8,128)(2,1)S(1)}, bf16[4,64,896]{2,1,0:T(8,128)(2,1)S(1)}, u32[]{:S(2)}, u32[]{:S(2)}) collective-permute-start(bf16[4,64,896]{2,1,0:T(8,128)(2,1)S(1)} %pad_maximum_fusion.1.refs_4_), channel_id=1, source_target_pairs={{2,0},{3,1},{0,2},{1,3},{6,4},{7,5},{4,6},{5,7},{10,8},{11,9},{8,1... | collective-permute-start | bytes 1376264 | tf_op jit(solution)/shard_map/ppermute | solution.py:31
  50.5 37.6 %collective-permute-start.11 = (bf16[4,64,896]{2,1,0:T(8,128)(2,1)S(1)}, bf16[4,64,896]{2,1,0:T(8,128)(2,1)S(1)}, u32[]{:S(2)}, u32[]{:S(2)}) collective-permute-start(bf16[4,64,896]{2,1,0:T(8,128)(2,1)S(1)} %pad_maximum_fusion.1.refs_4_), channel_id=1, source_target_pairs={{3,0},{0,1},{1,2},{2,3},{7,4},{4,5},{5,6},{6,7},{11,8},{8,9},{9,10... | collective-permute-start | bytes 1376264 | tf_op jit(solution)/shard_map/ppermute | solution.py:31
  51.8 37.2 %collective-permute-start.9 = (bf16[4,64,896]{2,1,0:T(8,128)(2,1)S(1)}, bf16[4,64,896]{2,1,0:T(8,128)(2,1)S(1)}, u32[]{:S(2)}, u32[]{:S(2)}) collective-permute-start(bf16[4,64,896]{2,1,0:T(8,128)(2,1)S(1)} %pad_maximum_fusion.1.refs_4_), channel_id=1, source_target_pairs={{1,0},{2,1},{3,2},{0,3},{5,4},{6,5},{7,6},{4,7},{9,8},{10,9},{11,1... | collective-permute-start | bytes 1376264 | tf_op jit(solution)/shard_map/ppermute | solution.py:31
  62.4 27.4 %collective-permute-start.3 = (bf16[4,64,896]{2,1,0:T(8,128)(2,1)S(1)}, bf16[4,64,896]{2,1,0:T(8,128)(2,1)S(1)}, u32[]{:S(2)}, u32[]{:S(2)}) collective-permute-start(bf16[4,64,896]{2,1,0:T(8,128)(2,1)S(1)} %pad_maximum_fusion.refs_0_), channel_id=1, source_target_pairs={{8,0},{16,8},{24,16},{0,24},{9,1},{17,9},{25,17},{1,25},{10,2},{18... | collective-permute-start | bytes 1376264 | tf_op jit(solution)/shard_map/ppermute | solution.py:31
  63.9 26.7 %collective-permute-start.4 = (bf16[4,64,896]{2,1,0:T(8,128)(2,1)S(1)}, bf16[4,64,896]{2,1,0:T(8,128)(2,1)S(1)}, u32[]{:S(2)}, u32[]{:S(2)}) collective-permute-start(bf16[4,64,896]{2,1,0:T(8,128)(2,1)S(1)} %pad_maximum_fusion.refs_0_), channel_id=1, source_target_pairs={{16,0},{24,8},{0,16},{8,24},{17,1},{25,9},{1,17},{9,25},{18,2},{26... | collective-permute-start | bytes 1376264 | tf_op jit(solution)/shard_map/ppermute | solution.py:31
  65.1 26.3 %collective-permute-start.5 = (bf16[4,64,896]{2,1,0:T(8,128)(2,1)S(1)}, bf16[4,64,896]{2,1,0:T(8,128)(2,1)}, u32[]{:S(2)}, u32[]{:S(2)}) collective-permute-start(bf16[4,64,896]{2,1,0:T(8,128)(2,1)S(1)} %pad_maximum_fusion.refs_0_), channel_id=1, source_target_pairs={{24,0},{0,8},{8,16},{16,24},{25,1},{1,9},{9,17},{17,25},{26,2},{2,... | collective-permute-start | bytes 1376264 | tf_op jit(solution)/shard_map/ppermute | solution.py:31
  76.2 26.8 %all-to-all-start.1 = ((bf16[64,8,225]{2,1,0:T(8,128)(2,1)}), bf16[64,8,225]{2,1,0:T(8,128)(2,1)S(1)}, u32[]{:S(2)}, u32[]{:S(2)}) async-start(bf16[64,8,225]{2,1,0:T(8,128)(2,1)} %reshape.176), calls=%async_computation.1 | async-start | bytes 524288 | tf_op jit(solution)/shard_map/all_to_all | solution.py:26
  107.9 14.2 %all-to-all-start.2 = ((f32[16,4,8,128]{3,2,1,0:T(8,128)}), f32[16,4,8,128]{3,2,1,0:T(8,128)S(1)}, u32[]{:S(2)}, u32[]{:S(2)}) async-start(f32[16,4,8,128]{3,2,1,0:T(8,128)} %get-tuple-element.29), calls=%async_computation.2 | async-start | bytes 524288 | tf_op jit(solution)/shard_map/all_to_all | solution.py:26
  132.3 3.6 %collective-permute-start.23 = (bf16[8,4,200,128]{3,2,1,0:T(8,128)(2,1)S(1)}, bf16[8,4,200,128]{3,2,1,0:T(8,128)(2,1)S(1)}, u32[]{:S(2)}, u32[]{:S(2)}) collective-permute-start(bf16[8,4,200,128]{3,2,1,0:T(8,128)(2,1)S(1)} %get-tuple-element.34), channel_id=1, source_target_pairs={{4,0},{0,4},{5,1},{1,5},{6,2},{2,6},{7,3},{3,7},{12,8},{8,12},{13,... | collective-permute-start | bytes 4915208 | tf_op jit(solution)/shard_map/ppermute | solution.py:31
  137.4 51.8 %copy-start.18 = (bf16[56,896]{1,0:T(8,128)(2,1)S(1)}, bf16[56,896]{1,0:T(8,128)(2,1)}, u32[]{:S(2)}) copy-start(bf16[56,896]{1,0:T(8,128)(2,1)} %two.1) | copy-start | bytes 301060
  137.5 51.8 %copy-start.19 = (bf16[56,896]{1,0:T(8,128)(2,1)S(1)}, bf16[56,896]{1,0:T(8,128)(2,1)}, u32[]{:S(2)}) copy-start(bf16[56,896]{1,0:T(8,128)(2,1)} %three.1) | copy-start | bytes 301060
  137.5 51.8 %copy-start.20 = (bf16[56,896]{1,0:T(8,128)(2,1)S(1)}, bf16[56,896]{1,0:T(8,128)(2,1)}, u32[]{:S(2)}) copy-start(bf16[56,896]{1,0:T(8,128)(2,1)} %four.1) | copy-start | bytes 301060
  137.5 53.4 %all-to-all-start.3 = ((bf16[32,200,128]{2,1,0:T(8,128)(2,1)}), bf16[32,200,128]{2,1,0:T(8,128)(2,1)S(1)}, u32[]{:S(2)}, u32[]{:S(2)}) async-start(bf16[32,200,128]{2,1,0:T(8,128)(2,1)} %bitcast.25), calls=%async_computation.3 | async-start | bytes 3276800 | tf_op jit(solution)/shard_map/all_to_all | solution.py:26
  147.1 1.3 collective-permute-start.15
  148.3 36.7 %collective-permute-start.16 = (f32[10,128]{1,0:T(8,128)S(1)}, f32[10,128]{1,0:T(8,128)S(1)}, u32[]{:S(2)}, u32[]{:S(2)}) collective-permute-start(f32[10,128]{1,0:T(8,128)S(1)} %fusion.3.refs_0_), channel_id=1, source_target_pairs={{32,0},{64,32},{96,64},{128,96},{160,128},{192,160},{224,192},{0,2... | collective-permute-start | bytes 15368 | tf_op jit(solution)/shard_map/ppermute | solution.py:31
  151.1 33.9 %collective-permute-start.17 = (f32[10,128]{1,0:T(8,128)S(1)}, f32[10,128]{1,0:T(8,128)S(1)}, u32[]{:S(2)}, u32[]{:S(2)}) collective-permute-start(f32[10,128]{1,0:T(8,128)S(1)} %fusion.3.refs_0_), channel_id=1, source_target_pairs={{64,0},{96,32},{128,64},{160,96},{192,128},{224,160},{0,192},{32,2... | collective-permute-start | bytes 15368 | tf_op jit(solution)/shard_map/ppermute | solution.py:31
  153.4 36.5 %collective-permute-start.18 = (f32[10,128]{1,0:T(8,128)S(1)}, f32[10,128]{1,0:T(8,128)S(1)}, u32[]{:S(2)}, u32[]{:S(2)}) collective-permute-start(f32[10,128]{1,0:T(8,128)S(1)} %fusion.3.refs_0_), channel_id=1, source_target_pairs={{96,0},{128,32},{160,64},{192,96},{224,128},{0,160},{32,192},{64,2... | collective-permute-start | bytes 15368 | tf_op jit(solution)/shard_map/ppermute | solution.py:31
  154.8 35.2 %collective-permute-start.19 = (f32[10,128]{1,0:T(8,128)S(1)}, f32[10,128]{1,0:T(8,128)S(1)}, u32[]{:S(2)}, u32[]{:S(2)}) collective-permute-start(f32[10,128]{1,0:T(8,128)S(1)} %fusion.3.refs_0_), channel_id=1, source_target_pairs={{128,0},{160,32},{192,64},{224,96},{0,128},{32,160},{64,192},{96,2... | collective-permute-start | bytes 15368 | tf_op jit(solution)/shard_map/ppermute | solution.py:31
  158.5 31.5 %collective-permute-start.20 = (f32[10,128]{1,0:T(8,128)S(1)}, f32[10,128]{1,0:T(8,128)S(1)}, u32[]{:S(2)}, u32[]{:S(2)}) collective-permute-start(f32[10,128]{1,0:T(8,128)S(1)} %fusion.3.refs_0_), channel_id=1, source_target_pairs={{160,0},{192,32},{224,64},{0,96},{32,128},{64,160},{96,192},{128,2... | collective-permute-start | bytes 15368 | tf_op jit(solution)/shard_map/ppermute | solution.py:31
  185.1 5.8 %collective-permute-start.21 = (f32[10,128]{1,0:T(8,128)S(1)}, f32[10,128]{1,0:T(8,128)S(1)}, u32[]{:S(2)}, u32[]{:S(2)}) collective-permute-start(f32[10,128]{1,0:T(8,128)S(1)} %fusion.3.refs_0_), channel_id=1, source_target_pairs={{192,0},{224,32},{0,64},{32,96},{64,128},{96,160},{128,192},{160,2... | collective-permute-start | bytes 15368 | tf_op jit(solution)/shard_map/ppermute | solution.py:31
  185.1 5.8 %collective-permute-start.22 = (f32[10,128]{1,0:T(8,128)S(1)}, f32[10,128]{1,0:T(8,128)S(1)}, u32[]{:S(2)}, u32[]{:S(2)}) collective-permute-start(f32[10,128]{1,0:T(8,128)S(1)} %fusion.3.refs_0_), channel_id=1, source_target_pairs={{224,0},{0,32},{32,64},{64,96},{96,128},{128,160},{160,192},{192,2... | collective-permute-start | bytes 15368 | tf_op jit(solution)/shard_map/ppermute | solution.py:31
  (21 other events, 152.0 us)
Sparse Core Ops, SparseCore 0:
  21.5 50.1 all-gather.1

commit v2 on v1

--- a/solution.py
+++ b/solution.py
@@ -67,12 +67,22 @@
         refs[YS][lax.rem(place[0] + r, YS)] = refs[r][...]
 
 
+def piece_copies(a_refs, b_refs, states, sems, xr):
+    slot_count = a_refs[0].shape[1]
+    found = []
+    for r in range(YS):
+        low = pl.ds(r * slot_count, slot_count)
+        high = pl.ds((YS + r) * slot_count, slot_count)
+        for part, (source, to) in enumerate(((a_refs[r].at[xr], low), (b_refs[xr].at[r], high))):
+            found.append(pltpu.make_async_copy(source, states.at[xr, to], sems.at[xr, r, part]))
+    return found
+
+
 def forward_kernel(place, *refs):
     a_refs, b_refs = refs[:YS], refs[YS : YS + XS]
-    weights, pre, held, sems = refs[YS + XS :]
+    weights, pre, states, held, sems, part_sems = refs[YS + XS :]
     x = place[1]
     heads_width = weights.shape[2]
-    half = pre.shape[0] // 2
     whole = heads_width // 256
 
     def loads(n):
@@ -85,22 +95,20 @@
             for xr in range(XS)
         ]
 
-    for n in range(whole + 1):
-        for copy in loads(n):
-            copy.start()
+    moves = [
+        copy for xr in range(XS) for copy in piece_copies(a_refs, b_refs, states, part_sems, xr)
+    ]
+    for copy in moves + [copy for n in range(whole + 1) for copy in loads(n)]:
+        copy.start()
+    for copy in moves:
+        copy.wait()
 
     def columns(n, at, wide):
-        total_a = total_b = None
+        total = None
         for xr in range(XS):
-            block = held[n, xr, :, :wide]
-            states_a = jnp.concatenate([a_refs[r][xr] for r in range(YS)], axis=0)
-            states_b = b_refs[xr][...].reshape(half, states_a.shape[1])
-            part_a = jnp.dot(states_a, block, preferred_element_type=f32)
-            part_b = jnp.dot(states_b, block, preferred_element_type=f32)
-            total_a = part_a if xr == 0 else total_a + part_a
-            total_b = part_b if xr == 0 else total_b + part_b
-        pre[:half, at] = total_a
-        pre[half:, at] = total_b
+            part = jnp.dot(states[xr], held[n, xr, :, :wide], preferred_element_type=f32)
+            total = part if xr == 0 else total + part
+        pre[:, at] = total
 
     @pl.loop(0, whole)
     def _(n):
@@ -115,7 +123,7 @@
     columns(whole, slice(whole * 256, heads_width), heads_width - whole * 256)
 
 
-def score_kernel(place, pre, back, extras, said, kept, embed):
+def score_kernel(place, pre, back, extras, said, kept, embed, sem):
     y = place[0]
     heads_width = pre.shape[1]
     cols = heads_width // 4
@@ -135,7 +143,8 @@
     ).astype(bf16)
     for h in range(4):
         embed[:, h * cols : (h + 1) * cols] = rows
-    kept[...] = embed[:, : kept.shape[1]]
+    keep = pltpu.make_async_copy(embed.at[:, : kept.shape[1]], kept, sem)
+    keep.start()
 
     @pl.loop(0, YS)
     def _(r):
@@ -158,22 +167,30 @@
         for copy in range(YS * XS):
             said[copy, lax.rem(y + r, YS)] = total
 
-
-def backward_kernel(place, bias, said, pre, embed, *refs):
+    keep.wait()
+
+
+def backward_kernel(place, bias, said, pre, embed_in, *refs):
     a_refs, b_refs = refs[:YS], refs[YS : YS + XS]
-    keep, send, small, value, held, grads = refs[YS + XS :]
+    keep, send, small, value = refs[YS + XS : YS + XS + 4]
+    states, embed, held, grads, sems, more = refs[YS + XS + 4 :]
+    fetch = pltpu.make_async_copy(embed_in, embed, more)
+    fetch.start()
+    loads = [piece_copies(a_refs, b_refs, states, sems, xr) for xr in range(XS)]
+    for load in sum(loads, []):
+        load.start()
     y, x, core = place[0], place[1], place[2]
     tokens = said.shape[4]
     slot_count = tokens // 2
     half = YS * slot_count
-    width = a_refs[0].shape[2]
+    width = states.shape[2]
     share = width // (ZS // XS * YS * CS)
     cols = width // YS
     both = 2 * cols
     slot = lax.rem(lax.broadcasted_iota(jnp.int32, (1, tokens), 1), tokens // 2).astype(f32)
     row = lax.broadcasted_iota(jnp.int32, (8, tokens), 0)
-    value[...] = jnp.zeros_like(value)
     bias_sum = loss_sum = count_sum = jnp.zeros((1, tokens), f32)
+    parts = []
     for r in range(YS):
         ya = lax.rem(y + r, YS)
         scores = said[0, 0, ya]
@@ -205,12 +222,10 @@
         third = e - first - second
         thirds = jnp.where(row == 0, first, jnp.where(row == 1, second, third))
         thirds = jnp.where(row < 3, thirds, 0.0).astype(bf16)
-        value[...] = (
-            value[...]
-            + jnp.dot(thirds[:, :slot_count], a_refs[r][0], preferred_element_type=f32)
-            + jnp.dot(thirds[:, slot_count:], b_refs[0][r], preferred_element_type=f32)
-        )
+        parts.append(thirds)
         upright = jnp.transpose(jnp.where(row == 0, g_one, jnp.where(row == 1, g_two, 0.0)))
+        if r == 0:
+            fetch.wait()
         for part in range(2):
             left = upright[part * slot_count : (part + 1) * slot_count, 0:1]
             right = upright[part * slot_count : (part + 1) * slot_count, 1:2]
@@ -230,15 +245,12 @@
         row == 0, bias_sum, jnp.where(row == 1, loss_sum, jnp.where(row == 2, count_sum, 0.0))
     )
 
-    def against(xr, states_b):
-        states_a = jnp.concatenate([ref[xr] for ref in a_refs], axis=0)
+    def against(xr):
         xa = lax.rem(x + xr, XS)
         for n in range(held.shape[1] // 256):
             lanes = slice(n * 256, (n + 1) * 256)
             grads[:, lanes] = lax.dot_general(
-                states_a, held[:half, lanes], (((0,), (0,)), ((), ())), preferred_element_type=f32
-            ) + lax.dot_general(
-                states_b, held[half:, lanes], (((0,), (0,)), ((), ())), preferred_element_type=f32
+                states[xr], held[:, lanes], (((0,), (0,)), ((), ())), preferred_element_type=f32
             )
         for z2 in range(ZS // XS):
             for yy in range(YS):
@@ -261,8 +273,25 @@
                     [theirs[:32], theirs[share - 32 :]], axis=1
                 ).astype(bf16)
 
-    for xr in range(XS):
-        against(xr, b_refs[xr][...].reshape(half, width))
+    for load in loads[0]:
+        load.wait()
+    total = jnp.zeros((8, width), f32)
+    for r, thirds in enumerate(parts):
+        for part in range(2):
+            at = part * half + r * slot_count
+            total = total + jnp.dot(
+                thirds[:, part * slot_count : (part + 1) * slot_count],
+                states[0, at : at + slot_count],
+                preferred_element_type=f32,
+            )
+    value[...] = total
+    against(0)
+    for load in sum(loads[1:], []):
+        load.wait()
+
+    @pl.loop(1, XS)
+    def _(xr):
+        against(xr)
 
 
 def finish_kernel(*refs):
@@ -372,29 +401,32 @@
         ]
     )
     group = YS * tokens
+    landed_parts = tuple(map(far, (*a_parts, *b_parts)))
     pre = pl.pallas_call(
         forward_kernel,
         out_shape=jax.ShapeDtypeStruct((group, 4 * cols), f32),
-        in_specs=[smem] + [vmem] * (YS + XS) + [anywhere],
+        in_specs=[smem] + [anywhere] * (YS + XS + 1),
         out_specs=vmem,
         scratch_shapes=[
+            VMEM((XS, group, width), bf16),
             VMEM((4 * cols // 256 + 1, XS, width, 256), bf16),
             pltpu.SemaphoreType.DMA((4 * cols // 256 + 1, XS)),
+            pltpu.SemaphoreType.DMA((XS, YS, 2)),
         ],
         compiler_params=limit,
         cost_estimate=pl.CostEstimate(
             flops=2 * group * XS * width * 4 * cols, bytes_accessed=12 << 20, transcendentals=0
         ),
-    )(place, *a_parts, *b_parts, far(weights))
+    )(place, *landed_parts, far(weights))
     said, embed = pl.pallas_call(
         score_kernel,
         out_shape=(
             jax.ShapeDtypeStruct((YS * XS, YS, 8, tokens), f32),
-            jax.ShapeDtypeStruct((group, 512), bf16),
+            pltpu.HBM((group, 512), bf16),
         ),
         in_specs=[smem] + [vmem] * 3,
-        out_specs=(vmem, vmem),
-        scratch_shapes=[VMEM((group, 4 * cols), bf16)],
+        out_specs=(vmem, anywhere),
+        scratch_shapes=[VMEM((group, 4 * cols), bf16), pltpu.SemaphoreType.DMA],
         compiler_params=limit,
     )(place, pre, back, extras)
 
@@ -408,14 +440,21 @@
             jax.ShapeDtypeStruct((8, tokens), f32),
             jax.ShapeDtypeStruct((8, width), f32),
         ),
-        in_specs=[smem, smem] + [vmem] * (3 + YS + XS),
+        in_specs=[smem, smem, vmem, vmem] + [anywhere] * (1 + YS + XS),
         out_specs=(vmem, vmem, vmem, vmem),
-        scratch_shapes=[VMEM((group, 512), bf16), VMEM((width, 512), f32)],
+        scratch_shapes=[
+            VMEM((XS, group, width), bf16),
+            VMEM((group, 512), bf16),
+            VMEM((group, 512), bf16),
+            VMEM((width, 512), f32),
+            pltpu.SemaphoreType.DMA((XS, YS, 2)),
+            pltpu.SemaphoreType.DMA,
+        ],
         compiler_params=limit,
         cost_estimate=pl.CostEstimate(
             flops=2 * group * XS * width * 512, bytes_accessed=12 << 20, transcendentals=0
         ),
-    )(place, value_bias, near(said), pre, embed, *a_parts, *b_parts)
+    )(place, value_bias, near(said), pre, far(embed), *landed_parts)
     terms = (keep + ahead(send, "c", 1).astype(f32)).astype(bf16)
     landed = exchange(terms.reshape(ZS * YS, *packed[2:]), ("z", "y")).reshape(packed)
 

time: 202 us -> 189 us (0.936)
  local copies, waits for them, and re-layouts: 27.5 us -> 11.7 us
  Pallas kernels: 20.8 us -> 26.2 us
    unnamed x49 -> x29, local copies, waits for them, and re-layouts: 15.6 us -> 2.21 us
    pallas_call x1, Pallas kernels: 4.01 us -> 7.11 us  [on_device(): pl.pallas_call(backward_kernel, out_shape=(VMEM(packed, f32), VMEM(packed...]
    pallas_call x1, Pallas kernels: 7.5 us -> 9.8 us  [on_device(): pl.pallas_call(forward_kernel, out_shape=jax.ShapeDtypeStruct((group, 4 *...]
  transfers between devices with their start and end apart: 29 -> 29, of which waited for: 9 -> 10; matrix products, arithmetic and copies ran while one was open for 9% -> 7% of each run, Pallas kernels for 4% -> 5%
where the time goes in v2:
time: 189 us; the launch traced here: 188 us
  starting transfers between devices  76.1 us (40%)
  waiting for transfers between devices  50.8 us (27%)
  Pallas kernels  26.2 us (14%)
  between operations  15 us (8%)
  local copies, waits for them, and re-layouts  11.7 us (6%)
  other arithmetic  7.64 us (4%)
    ppermute x24, waiting for transfers between devices, ahead(): lax.ppermute(a, axis, tuple((((i + steps) % n, i) for i in range(n))))  43.3 us
    ppermute x24, starting transfers between devices, ahead(): lax.ppermute(a, axis, tuple((((i + steps) % n, i) for i in range(n))))  38.1 us
    all_to_all x4, starting transfers between devices, exchange(): return lax.all_to_all(pieces, axes, split_axis=0, concat_axis=0, tiled=True)  38 us
    pallas_call x1, Pallas kernels, on_device(): pl.pallas_call(forward_kernel, out_shape=jax.ShapeDtypeStruct((group, 4 *...  9.8 us
    all_to_all x4, waiting for transfers between devices, exchange(): return lax.all_to_all(pieces, axes, split_axis=0, concat_axis=0, tiled=True)  7.53 us
    pallas_call x1, Pallas kernels, on_device(): pl.pallas_call(backward_kernel, out_shape=(VMEM(packed, f32), VMEM(packed...  7.11 us
    pallas_call x1, Pallas kernels, on_device(): pl.pallas_call(score_kernel, out_shape=(jax.ShapeDtypeStruct((YS * XS, YS...  4.12 us
    gather x1, local copies, waits for them, and re-layouts, lookup(): found = table[got & 4095]  3.81 us
  transfers between devices with their start and end apart: 29, of which 10 were waited for; matrix products, arithmetic and copies ran while one was open for 7% of the time, Pallas kernels for 5%

profile of v2, /device:TPU:8, one launch (start us, length us, event | category | flops | bytes accessed | tf_op | source)
XLA Modules:
  0.0 187.6 jit_solution(14180915610054928409)
XLA Ops:
  7.8 2.2 %shard_map.162 = (bf16[56,896]{1,0:T(8,128)(2,1)}, bf16[56,896]{1,0:T(8,128)(2,1)}, bf16[56,896]{1,0:T(8,128)(2,1)}, bf16[56,896]{1,0:T(8,128)(2,1)}, bf16[64,896]{1,0:T(8,128)(2,1)}, /*index=5*/bf16[64,896]{1,0:T(8,128)(2,1)}) custom-call(s32[3]{0:T(128)} %pad_add_fusion.place, bf16[56,896]{1,0:T(8,128)(2,1)} %one.1, bf16[56,896]{1,0:T(8,128)(2,1)} %two.1, ...), custom_call_target="tpu_custom_call" | custom-call | tf_op jit(solution)/shard_map/pallas_call | solution.py:367
  10.0 2.2 %collective-permute-start.12 = (bf16[56,896]{1,0:T(8,128)(2,1)}, bf16[56,896]{1,0:T(8,128)(2,1)S(1)}, u32[]{:S(2)}, u32[]{:S(2)}) collective-permute-start(bf16[56,896]{1,0:T(8,128)(2,1)} %get-tuple-element.26), channel_id=1, source_target_pairs={{8,0},{16,8},{24,16},{0,24},{9,1},{17,9},{25,17},{1,25},{10,2},{18... | collective-permute-start | bytes 301064 | tf_op jit(solution)/shard_map/ppermute | solution.py:31
  13.1 1.9 %collective-permute-start.14 = (bf16[56,896]{1,0:T(8,128)(2,1)}, bf16[56,896]{1,0:T(8,128)(2,1)S(1)}, u32[]{:S(2)}, u32[]{:S(2)}) collective-permute-start(bf16[56,896]{1,0:T(8,128)(2,1)} %get-tuple-element.28), channel_id=1, source_target_pairs={{24,0},{0,8},{8,16},{16,24},{25,1},{1,9},{9,17},{17,25},{26,2},{2,... | collective-permute-start | bytes 301064 | tf_op jit(solution)/shard_map/ppermute | solution.py:31
  15.2 3.3 %collective-permute-done.13.refs_2_ = bf16[56,896]{1,0:T(8,128)(2,1)S(1)} collective-permute-done((bf16[56,896]{1,0:T(8,128)(2,1)}, bf16[56,896]{1,0:T(8,128)(2,1)S(1)}, u32[]{:S(2)}, u32[]{:S(2)}) %collective-permute-start.13) | collective-permute-done | bytes 100384 | tf_op jit(solution)/shard_map/ppermute | solution.py:31
  19.4 1.8 shard_map.163
  24.0 12.0 %all-to-all-start = ((s32[64,1,2]{2,1,0:T(1,128)}), s32[64,1,2]{2,1,0:T(1,128)S(1)}, u32[]{:S(2)}, u32[]{:S(2)}) async-start(s32[64,1,2]{2,1,0:T(1,128)} %bitcast.13), calls=%async_computation | async-start | bytes 65536 | tf_op jit(solution)/shard_map/all_to_all | solution.py:26
  36.0 1.5 collective-permute-start.8
  38.1 2.1 %collective-permute-start.7 = (bf16[64,896]{1,0:T(8,128)(2,1)}, bf16[64,896]{1,0:T(8,128)(2,1)S(1)}, u32[]{:S(2)}, u32[]{:S(2)}) collective-permute-start(bf16[64,896]{1,0:T(8,128)(2,1)} %get-tuple-element.24), channel_id=1, source_target_pairs={{16,0},{24,8},{0,16},{8,24},{17,1},{25,9},{1,17},{9,25},{18,2},{26... | collective-permute-start | bytes 344072 | tf_op jit(solution)/shard_map/ppermute | solution.py:31
  40.2 2.8 %collective-permute-start = (bf16[64,896]{1,0:T(8,128)(2,1)}, bf16[64,896]{1,0:T(8,128)(2,1)S(1)}, u32[]{:S(2)}, u32[]{:S(2)}) collective-permute-start(bf16[64,896]{1,0:T(8,128)(2,1)} %get-tuple-element.23), channel_id=1, source_target_pairs={{1,0},{2,1},{3,2},{0,3},{5,4},{6,5},{7,6},{4,7},{9,8},{10,9},{11,1... | collective-permute-start | bytes 344072 | tf_op jit(solution)/shard_map/ppermute | solution.py:31
  48.1 2.2 %collective-permute-start.10 = (bf16[4,64,896]{2,1,0:T(8,128)(2,1)S(1)}, bf16[4,64,896]{2,1,0:T(8,128)(2,1)S(1)}, u32[]{:S(2)}, u32[]{:S(2)}) collective-permute-start(bf16[4,64,896]{2,1,0:T(8,128)(2,1)S(1)} %pad_maximum_fusion.1.refs_4_), channel_id=1, source_target_pairs={{2,0},{3,1},{0,2},{1,3},{6,4},{7,5},{4,6},{5,7},{10,8},{11,9},{8,1... | collective-permute-start | bytes 1376264 | tf_op jit(solution)/shard_map/ppermute | solution.py:31
  50.5 1.2 collective-permute-start.11
  51.7 2.1 %collective-permute-start.9 = (bf16[4,64,896]{2,1,0:T(8,128)(2,1)S(1)}, bf16[4,64,896]{2,1,0:T(8,128)(2,1)S(1)}, u32[]{:S(2)}, u32[]{:S(2)}) collective-permute-start(bf16[4,64,896]{2,1,0:T(8,128)(2,1)S(1)} %pad_maximum_fusion.1.refs_4_), channel_id=1, source_target_pairs={{1,0},{2,1},{3,2},{0,3},{5,4},{6,5},{7,6},{4,7},{9,8},{10,9},{11,1... | collective-permute-start | bytes 1376264 | tf_op jit(solution)/shard_map/ppermute | solution.py:31
  53.8 7.6 %collective-permute-done.2 = bf16[64,896]{1,0:T(8,128)(2,1)S(1)} collective-permute-done((bf16[64,896]{1,0:T(8,128)(2,1)}, bf16[64,896]{1,0:T(8,128)(2,1)S(1)}, u32[]{:S(2)}, u32[]{:S(2)}) %collective-permute-start.2) | collective-permute-done | bytes 114720 | tf_op jit(solution)/shard_map/ppermute | solution.py:31
  62.4 1.5 collective-permute-start.3
  65.1 1.6 collective-permute-start.5
  66.7 3.8 %gather_fusion = bf16[128,896]{1,0:T(8,128)(2,1)S(1)} fusion(bf16[2376,896]{1,0:T(8,128)(2,1)} %param.15, s32[1024]{0:T(1024)S(1)} %pad_clamp_fusion), kind=kCustom, calls=%fused_computation | custom fusion | bytes 459264 | tf_op jit(solution)/shard_map/gather | solution.py:337
  72.8 10.6 %all-to-all-start.1 = ((bf16[64,8,225]{2,1,0:T(8,128)(2,1)}), bf16[64,8,225]{2,1,0:T(8,128)(2,1)S(1)}, u32[]{:S(2)}, u32[]{:S(2)}) async-start(bf16[64,8,225]{2,1,0:T(8,128)(2,1)} %reshape.176), calls=%async_computation.1 | async-start | bytes 524288 | tf_op jit(solution)/shard_map/all_to_all | solution.py:26
  84.7 9.8 %shard_map.164.pre = f32[512,896]{1,0:T(8,128)S(1)} custom-call(s32[3]{0:T(128)S(1)} %copy-done, bf16[4,64,896]{2,1,0:T(8,128)(2,1)} %copy-done.3, bf16[4,64,896]{2,1,0:T(8,128)(2,1)} %collective-permute-done.3.refs_1_, bf16[4,64,896]{2,1,0:T(8,128)(2,1)} %collective-permute-done.4.refs_2_, bf16[4,64,896]{2,1,0:T(8,128)(2,1)} %collective-permute-done.5.refs_3_, ...), custom_call_target="tpu_custom_call" | custom-call | flops 3288334336 | bytes 12582912 | tf_op jit(solution)/shard_map/pallas_call | solution.py:405
  95.7 4.1 %shard_map.165 = (f32[16,4,8,128]{3,2,1,0:T(8,128)}, bf16[512,512]{1,0:T(8,128)(2,1)}) custom-call(s32[3]{0:T(128)S(1)} %copy-done, f32[512,896]{1,0:T(8,128)S(1)} %shard_map.164.pre, bf16[512,225]{1,0:T(8,128)(2,1)S(1)} %bitcast.41, f32[8,128]{1,0:T(8,128)S(1)} %concatenate.10.extras), custom_call_target="tpu_custom_call" | custom-call | tf_op jit(solution)/shard_map/pallas_call | solution.py:421
  99.8 6.8 %all-to-all-start.2 = ((f32[16,4,8,128]{3,2,1,0:T(8,128)}), f32[16,4,8,128]{3,2,1,0:T(8,128)S(1)}, u32[]{:S(2)}, u32[]{:S(2)}) async-start(f32[16,4,8,128]{3,2,1,0:T(8,128)} %get-tuple-element.29), calls=%async_computation.2 | async-start | bytes 524288 | tf_op jit(solution)/shard_map/all_to_all | solution.py:26
  107.2 6.3 %all-to-all-done.2 = f32[16,4,8,128]{3,2,1,0:T(8,128)S(1)} async-done(((f32[16,4,8,128]{3,2,1,0:T(8,128)}), f32[16,4,8,128]{3,2,1,0:T(8,128)S(1)}, u32[]{:S(2)}, u32[]{:S(2)}) %all-to-all-start.2) | async-done | bytes 262176 | tf_op jit(solution)/shard_map/all_to_all | solution.py:26
  113.6 7.1 %shard_map.166 = (f32[8,4,200,128]{3,2,1,0:T(8,128)S(1)}, bf16[8,4,200,128]{3,2,1,0:T(8,128)(2,1)S(1)}, f32[8,128]{1,0:T(8,128)S(1)}, f32[8,896]{1,0:T(8,128)S(1)}) custom-call(s32[3]{0:T(128)S(1)} %copy-done, f32[1]{0:T(128)S(6)} %copy.51.bias, f32[4,4,4,8,128]{4,3,2,1,0:T(8,128)S(1)} %bitcast.42, f32[512,896]{1,0:T(8,128)S(1)} %shard_map.164.pre, ...), custom_call_target="tpu_custom_call" | custom-call | flops 1879048192 | bytes 12582912 | tf_op jit(solution)/shard_map/pallas_call | solution.py:435
  120.8 3.5 %collective-permute-done.23 = bf16[8,4,200,128]{3,2,1,0:T(8,128)(2,1)S(1)} collective-permute-done((bf16[8,4,200,128]{3,2,1,0:T(8,128)(2,1)S(1)}, bf16[8,4,200,128]{3,2,1,0:T(8,128)(2,1)S(1)}, u32[]{:S(2)}, u32[]{:S(2)}) %collective-permute-start.23) | collective-permute-done | bytes 1638432 | tf_op jit(solution)/shard_map/ppermute | solution.py:31
  124.3 1.6 add_convert_fusion
  125.9 8.5 %all-to-all-start.3 = ((bf16[32,200,128]{2,1,0:T(8,128)(2,1)}), bf16[32,200,128]{2,1,0:T(8,128)(2,1)S(1)}, u32[]{:S(2)}, u32[]{:S(2)}) async-start(bf16[32,200,128]{2,1,0:T(8,128)(2,1)} %bitcast.25), calls=%async_computation.3 | async-start | bytes 3276800 | tf_op jit(solution)/shard_map/all_to_all | solution.py:26
  136.0 2.8 %collective-permute-start.16 = (f32[10,128]{1,0:T(8,128)S(1)}, f32[10,128]{1,0:T(8,128)S(1)}, u32[]{:S(2)}, u32[]{:S(2)}) collective-permute-start(f32[10,128]{1,0:T(8,128)S(1)} %fusion.3.refs_0_), channel_id=1, source_target_pairs={{32,0},{64,32},{96,64},{128,96},{160,128},{192,160},{224,192},{0,2... | collective-permute-start | bytes 15368 | tf_op jit(solution)/shard_map/ppermute | solution.py:31
  138.7 2.3 %collective-permute-start.17 = (f32[10,128]{1,0:T(8,128)S(1)}, f32[10,128]{1,0:T(8,128)S(1)}, u32[]{:S(2)}, u32[]{:S(2)}) collective-permute-start(f32[10,128]{1,0:T(8,128)S(1)} %fusion.3.refs_0_), channel_id=1, source_target_pairs={{64,0},{96,32},{128,64},{160,96},{192,128},{224,160},{0,192},{32,2... | collective-permute-start | bytes 15368 | tf_op jit(solution)/shard_map/ppermute | solution.py:31
  141.0 1.4 collective-permute-start.18
  142.5 3.6 %collective-permute-start.19 = (f32[10,128]{1,0:T(8,128)S(1)}, f32[10,128]{1,0:T(8,128)S(1)}, u32[]{:S(2)}, u32[]{:S(2)}) collective-permute-start(f32[10,128]{1,0:T(8,128)S(1)} %fusion.3.refs_0_), channel_id=1, source_target_pairs={{128,0},{160,32},{192,64},{224,96},{0,128},{32,160},{64,192},{96,2... | collective-permute-start | bytes 15368 | tf_op jit(solution)/shard_map/ppermute | solution.py:31
  146.3 26.4 %collective-permute-done.16.refs_1_ = f32[10,128]{1,0:T(8,128)S(1)} collective-permute-done((f32[10,128]{1,0:T(8,128)S(1)}, f32[10,128]{1,0:T(8,128)S(1)}, u32[]{:S(2)}, u32[]{:S(2)}) %collective-permute-start.16) | collective-permute-done | bytes 5152 | tf_op jit(solution)/shard_map/ppermute | solution.py:31
  172.7 4.2 %collective-permute-start.22 = (f32[10,128]{1,0:T(8,128)S(1)}, f32[10,128]{1,0:T(8,128)S(1)}, u32[]{:S(2)}, u32[]{:S(2)}) collective-permute-start(f32[10,128]{1,0:T(8,128)S(1)} %fusion.3.refs_0_), channel_id=1, source_target_pairs={{224,0},{0,32},{32,64},{64,96},{96,128},{128,160},{160,192},{192,2... | collective-permute-start | bytes 15368 | tf_op jit(solution)/shard_map/ppermute | solution.py:31
  179.5 1.3 fusion.4
  (107 shorter events, 22.4 us)
Async XLA Ops:
  7.2 76.6 %all-gather.2.cloned.1.call-start = ((), (), s32[]{:S(2)}) async-start(), calls=%async_computation.4 | async-start | bytes 6823936 | tf_op jit(solution)/shard_map/all_gather | solution.py:381
  10.0 5.2 %collective-permute-start.12 = (bf16[56,896]{1,0:T(8,128)(2,1)}, bf16[56,896]{1,0:T(8,128)(2,1)S(1)}, u32[]{:S(2)}, u32[]{:S(2)}) collective-permute-start(bf16[56,896]{1,0:T(8,128)(2,1)} %get-tuple-element.26), channel_id=1, source_target_pairs={{8,0},{16,8},{24,16},{0,24},{9,1},{17,9},{25,17},{1,25},{10,2},{18... | collective-permute-start | bytes 301064 | tf_op jit(solution)/shard_map/ppermute | solution.py:31
  12.2 6.4 %collective-permute-start.13 = (bf16[56,896]{1,0:T(8,128)(2,1)}, bf16[56,896]{1,0:T(8,128)(2,1)S(1)}, u32[]{:S(2)}, u32[]{:S(2)}) collective-permute-start(bf16[56,896]{1,0:T(8,128)(2,1)} %get-tuple-element.27), channel_id=1, source_target_pairs={{16,0},{24,8},{0,16},{8,24},{17,1},{25,9},{1,17},{9,25},{18,2},{26... | collective-permute-start | bytes 301064 | tf_op jit(solution)/shard_map/ppermute | solution.py:31
  13.1 5.7 %collective-permute-start.14 = (bf16[56,896]{1,0:T(8,128)(2,1)}, bf16[56,896]{1,0:T(8,128)(2,1)S(1)}, u32[]{:S(2)}, u32[]{:S(2)}) collective-permute-start(bf16[56,896]{1,0:T(8,128)(2,1)} %get-tuple-element.28), channel_id=1, source_target_pairs={{24,0},{0,8},{8,16},{16,24},{25,1},{1,9},{9,17},{17,25},{26,2},{2,... | collective-permute-start | bytes 301064 | tf_op jit(solution)/shard_map/ppermute | solution.py:31
  24.0 22.0 %all-to-all-start = ((s32[64,1,2]{2,1,0:T(1,128)}), s32[64,1,2]{2,1,0:T(1,128)S(1)}, u32[]{:S(2)}, u32[]{:S(2)}) async-start(s32[64,1,2]{2,1,0:T(1,128)} %bitcast.13), calls=%async_computation | async-start | bytes 65536 | tf_op jit(solution)/shard_map/all_to_all | solution.py:26
  36.0 10.1 %collective-permute-start.8 = (bf16[64,896]{1,0:T(8,128)(2,1)}, bf16[64,896]{1,0:T(8,128)(2,1)S(1)}, u32[]{:S(2)}, u32[]{:S(2)}) collective-permute-start(bf16[64,896]{1,0:T(8,128)(2,1)} %get-tuple-element.24), channel_id=1, source_target_pairs={{24,0},{0,8},{8,16},{16,24},{25,1},{1,9},{9,17},{17,25},{26,2},{2,... | collective-permute-start | bytes 344072 | tf_op jit(solution)/shard_map/ppermute | solution.py:31
  37.6 9.5 %collective-permute-start.6 = (bf16[64,896]{1,0:T(8,128)(2,1)}, bf16[64,896]{1,0:T(8,128)(2,1)S(1)}, u32[]{:S(2)}, u32[]{:S(2)}) collective-permute-start(bf16[64,896]{1,0:T(8,128)(2,1)} %get-tuple-element.24), channel_id=1, source_target_pairs={{8,0},{16,8},{24,16},{0,24},{9,1},{17,9},{25,17},{1,25},{10,2},{18... | collective-permute-start | bytes 344072 | tf_op jit(solution)/shard_map/ppermute | solution.py:31
  38.1 9.0 %collective-permute-start.7 = (bf16[64,896]{1,0:T(8,128)(2,1)}, bf16[64,896]{1,0:T(8,128)(2,1)S(1)}, u32[]{:S(2)}, u32[]{:S(2)}) collective-permute-start(bf16[64,896]{1,0:T(8,128)(2,1)} %get-tuple-element.24), channel_id=1, source_target_pairs={{16,0},{24,8},{0,16},{8,24},{17,1},{25,9},{1,17},{9,25},{18,2},{26... | collective-permute-start | bytes 344072 | tf_op jit(solution)/shard_map/ppermute | solution.py:31
  40.2 11.5 %collective-permute-start = (bf16[64,896]{1,0:T(8,128)(2,1)}, bf16[64,896]{1,0:T(8,128)(2,1)S(1)}, u32[]{:S(2)}, u32[]{:S(2)}) collective-permute-start(bf16[64,896]{1,0:T(8,128)(2,1)} %get-tuple-element.23), channel_id=1, source_target_pairs={{1,0},{2,1},{3,2},{0,3},{5,4},{6,5},{7,6},{4,7},{9,8},{10,9},{11,1... | collective-permute-start | bytes 344072 | tf_op jit(solution)/shard_map/ppermute | solution.py:31
  42.9 10.9 %collective-permute-start.1 = (bf16[64,896]{1,0:T(8,128)(2,1)}, bf16[64,896]{1,0:T(8,128)(2,1)S(1)}, u32[]{:S(2)}, u32[]{:S(2)}) collective-permute-start(bf16[64,896]{1,0:T(8,128)(2,1)} %get-tuple-element.23), channel_id=1, source_target_pairs={{2,0},{3,1},{0,2},{1,3},{6,4},{7,5},{4,6},{5,7},{10,8},{11,9},{8,1... | collective-permute-start | bytes 344072 | tf_op jit(solution)/shard_map/ppermute | solution.py:31
  46.1 15.3 %collective-permute-start.2 = (bf16[64,896]{1,0:T(8,128)(2,1)}, bf16[64,896]{1,0:T(8,128)(2,1)S(1)}, u32[]{:S(2)}, u32[]{:S(2)}) collective-permute-start(bf16[64,896]{1,0:T(8,128)(2,1)} %get-tuple-element.23), channel_id=1, source_target_pairs={{3,0},{0,1},{1,2},{2,3},{7,4},{4,5},{5,6},{6,7},{11,8},{8,9},{9,10... | collective-permute-start | bytes 344072 | tf_op jit(solution)/shard_map/ppermute | solution.py:31
  48.1 17.0 %collective-permute-start.10 = (bf16[4,64,896]{2,1,0:T(8,128)(2,1)S(1)}, bf16[4,64,896]{2,1,0:T(8,128)(2,1)S(1)}, u32[]{:S(2)}, u32[]{:S(2)}) collective-permute-start(bf16[4,64,896]{2,1,0:T(8,128)(2,1)S(1)} %pad_maximum_fusion.1.refs_4_), channel_id=1, source_target_pairs={{2,0},{3,1},{0,2},{1,3},{6,4},{7,5},{4,6},{5,7},{10,8},{11,9},{8,1... | collective-permute-start | bytes 1376264 | tf_op jit(solution)/shard_map/ppermute | solution.py:31
  50.5 33.2 %collective-permute-start.11 = (bf16[4,64,896]{2,1,0:T(8,128)(2,1)S(1)}, bf16[4,64,896]{2,1,0:T(8,128)(2,1)S(1)}, u32[]{:S(2)}, u32[]{:S(2)}) collective-permute-start(bf16[4,64,896]{2,1,0:T(8,128)(2,1)S(1)} %pad_maximum_fusion.1.refs_4_), channel_id=1, source_target_pairs={{3,0},{0,1},{1,2},{2,3},{7,4},{4,5},{5,6},{6,7},{11,8},{8,9},{9,10... | collective-permute-start | bytes 1376264 | tf_op jit(solution)/shard_map/ppermute | solution.py:31
  51.7 32.0 %collective-permute-start.9 = (bf16[4,64,896]{2,1,0:T(8,128)(2,1)S(1)}, bf16[4,64,896]{2,1,0:T(8,128)(2,1)S(1)}, u32[]{:S(2)}, u32[]{:S(2)}) collective-permute-start(bf16[4,64,896]{2,1,0:T(8,128)(2,1)S(1)} %pad_maximum_fusion.1.refs_4_), channel_id=1, source_target_pairs={{1,0},{2,1},{3,2},{0,3},{5,4},{6,5},{7,6},{4,7},{9,8},{10,9},{11,1... | collective-permute-start | bytes 1376264 | tf_op jit(solution)/shard_map/ppermute | solution.py:31
  62.4 21.4 %collective-permute-start.3 = (bf16[4,64,896]{2,1,0:T(8,128)(2,1)S(1)}, bf16[4,64,896]{2,1,0:T(8,128)(2,1)}, u32[]{:S(2)}, u32[]{:S(2)}) collective-permute-start(bf16[4,64,896]{2,1,0:T(8,128)(2,1)S(1)} %pad_maximum_fusion.refs_0_), channel_id=1, source_target_pairs={{8,0},{16,8},{24,16},{0,24},{9,1},{17,9},{25,17},{1,25},{10,2},{18... | collective-permute-start | bytes 1376264 | tf_op jit(solution)/shard_map/ppermute | solution.py:31
  63.9 19.9 %collective-permute-start.4 = (bf16[4,64,896]{2,1,0:T(8,128)(2,1)S(1)}, bf16[4,64,896]{2,1,0:T(8,128)(2,1)}, u32[]{:S(2)}, u32[]{:S(2)}) collective-permute-start(bf16[4,64,896]{2,1,0:T(8,128)(2,1)S(1)} %pad_maximum_fusion.refs_0_), channel_id=1, source_target_pairs={{16,0},{24,8},{0,16},{8,24},{17,1},{25,9},{1,17},{9,25},{18,2},{26... | collective-permute-start | bytes 1376264 | tf_op jit(solution)/shard_map/ppermute | solution.py:31
  65.1 18.7 %collective-permute-start.5 = (bf16[4,64,896]{2,1,0:T(8,128)(2,1)S(1)}, bf16[4,64,896]{2,1,0:T(8,128)(2,1)}, u32[]{:S(2)}, u32[]{:S(2)}) collective-permute-start(bf16[4,64,896]{2,1,0:T(8,128)(2,1)S(1)} %pad_maximum_fusion.refs_0_), channel_id=1, source_target_pairs={{24,0},{0,8},{8,16},{16,24},{25,1},{1,9},{9,17},{17,25},{26,2},{2,... | collective-permute-start | bytes 1376264 | tf_op jit(solution)/shard_map/ppermute | solution.py:31
  72.8 22.8 %all-to-all-start.1 = ((bf16[64,8,225]{2,1,0:T(8,128)(2,1)}), bf16[64,8,225]{2,1,0:T(8,128)(2,1)S(1)}, u32[]{:S(2)}, u32[]{:S(2)}) async-start(bf16[64,8,225]{2,1,0:T(8,128)(2,1)} %reshape.176), calls=%async_computation.1 | async-start | bytes 524288 | tf_op jit(solution)/shard_map/all_to_all | solution.py:26
  99.8 13.8 %all-to-all-start.2 = ((f32[16,4,8,128]{3,2,1,0:T(8,128)}), f32[16,4,8,128]{3,2,1,0:T(8,128)S(1)}, u32[]{:S(2)}, u32[]{:S(2)}) async-start(f32[16,4,8,128]{3,2,1,0:T(8,128)} %get-tuple-element.29), calls=%async_computation.2 | async-start | bytes 524288 | tf_op jit(solution)/shard_map/all_to_all | solution.py:26
  120.7 3.6 %collective-permute-start.23 = (bf16[8,4,200,128]{3,2,1,0:T(8,128)(2,1)S(1)}, bf16[8,4,200,128]{3,2,1,0:T(8,128)(2,1)S(1)}, u32[]{:S(2)}, u32[]{:S(2)}) collective-permute-start(bf16[8,4,200,128]{3,2,1,0:T(8,128)(2,1)S(1)} %get-tuple-element.34), channel_id=1, source_target_pairs={{4,0},{0,4},{5,1},{1,5},{6,2},{2,6},{7,3},{3,7},{12,8},{8,12},{13,... | collective-permute-start | bytes 4915208 | tf_op jit(solution)/shard_map/ppermute | solution.py:31
  125.9 51.0 %copy-start.5 = (bf16[56,896]{1,0:T(8,128)(2,1)S(1)}, bf16[56,896]{1,0:T(8,128)(2,1)}, u32[]{:S(2)}) copy-start(bf16[56,896]{1,0:T(8,128)(2,1)} %two.1) | copy-start | bytes 301060
  125.9 51.0 %copy-start.6 = (bf16[56,896]{1,0:T(8,128)(2,1)S(1)}, bf16[56,896]{1,0:T(8,128)(2,1)}, u32[]{:S(2)}) copy-start(bf16[56,896]{1,0:T(8,128)(2,1)} %three.1) | copy-start | bytes 301060
  125.9 51.0 %copy-start.7 = (bf16[56,896]{1,0:T(8,128)(2,1)S(1)}, bf16[56,896]{1,0:T(8,128)(2,1)}, u32[]{:S(2)}) copy-start(bf16[56,896]{1,0:T(8,128)(2,1)} %four.1) | copy-start | bytes 301060
  125.9 52.5 %all-to-all-start.3 = ((bf16[32,200,128]{2,1,0:T(8,128)(2,1)}), bf16[32,200,128]{2,1,0:T(8,128)(2,1)S(1)}, u32[]{:S(2)}, u32[]{:S(2)}) async-start(bf16[32,200,128]{2,1,0:T(8,128)(2,1)} %bitcast.25), calls=%async_computation.3 | async-start | bytes 3276800 | tf_op jit(solution)/shard_map/all_to_all | solution.py:26
  134.7 1.3 collective-permute-start.15
  136.0 36.7 %collective-permute-start.16 = (f32[10,128]{1,0:T(8,128)S(1)}, f32[10,128]{1,0:T(8,128)S(1)}, u32[]{:S(2)}, u32[]{:S(2)}) collective-permute-start(f32[10,128]{1,0:T(8,128)S(1)} %fusion.3.refs_0_), channel_id=1, source_target_pairs={{32,0},{64,32},{96,64},{128,96},{160,128},{192,160},{224,192},{0,2... | collective-permute-start | bytes 15368 | tf_op jit(solution)/shard_map/ppermute | solution.py:31
  138.7 34.0 %collective-permute-start.17 = (f32[10,128]{1,0:T(8,128)S(1)}, f32[10,128]{1,0:T(8,128)S(1)}, u32[]{:S(2)}, u32[]{:S(2)}) collective-permute-start(f32[10,128]{1,0:T(8,128)S(1)} %fusion.3.refs_0_), channel_id=1, source_target_pairs={{64,0},{96,32},{128,64},{160,96},{192,128},{224,160},{0,192},{32,2... | collective-permute-start | bytes 15368 | tf_op jit(solution)/shard_map/ppermute | solution.py:31
  141.0 36.6 %collective-permute-start.18 = (f32[10,128]{1,0:T(8,128)S(1)}, f32[10,128]{1,0:T(8,128)S(1)}, u32[]{:S(2)}, u32[]{:S(2)}) collective-permute-start(f32[10,128]{1,0:T(8,128)S(1)} %fusion.3.refs_0_), channel_id=1, source_target_pairs={{96,0},{128,32},{160,64},{192,96},{224,128},{0,160},{32,192},{64,2... | collective-permute-start | bytes 15368 | tf_op jit(solution)/shard_map/ppermute | solution.py:31
  142.5 35.2 %collective-permute-start.19 = (f32[10,128]{1,0:T(8,128)S(1)}, f32[10,128]{1,0:T(8,128)S(1)}, u32[]{:S(2)}, u32[]{:S(2)}) collective-permute-start(f32[10,128]{1,0:T(8,128)S(1)} %fusion.3.refs_0_), channel_id=1, source_target_pairs={{128,0},{160,32},{192,64},{224,96},{0,128},{32,160},{64,192},{96,2... | collective-permute-start | bytes 15368 | tf_op jit(solution)/shard_map/ppermute | solution.py:31
  146.1 31.5 %collective-permute-start.20 = (f32[10,128]{1,0:T(8,128)S(1)}, f32[10,128]{1,0:T(8,128)S(1)}, u32[]{:S(2)}, u32[]{:S(2)}) collective-permute-start(f32[10,128]{1,0:T(8,128)S(1)} %fusion.3.refs_0_), channel_id=1, source_target_pairs={{160,0},{192,32},{224,64},{0,96},{32,128},{64,160},{96,192},{128,2... | collective-permute-start | bytes 15368 | tf_op jit(solution)/shard_map/ppermute | solution.py:31
  172.7 5.8 %collective-permute-start.21 = (f32[10,128]{1,0:T(8,128)S(1)}, f32[10,128]{1,0:T(8,128)S(1)}, u32[]{:S(2)}, u32[]{:S(2)}) collective-permute-start(f32[10,128]{1,0:T(8,128)S(1)} %fusion.3.refs_0_), channel_id=1, source_target_pairs={{192,0},{224,32},{0,64},{32,96},{64,128},{96,160},{128,192},{160,2... | collective-permute-start | bytes 15368 | tf_op jit(solution)/shard_map/ppermute | solution.py:31
  172.7 5.8 %collective-permute-start.22 = (f32[10,128]{1,0:T(8,128)S(1)}, f32[10,128]{1,0:T(8,128)S(1)}, u32[]{:S(2)}, u32[]{:S(2)}) collective-permute-start(f32[10,128]{1,0:T(8,128)S(1)} %fusion.3.refs_0_), channel_id=1, source_target_pairs={{224,0},{0,32},{32,64},{64,96},{96,128},{128,160},{160,192},{192,2... | collective-permute-start | bytes 15368 | tf_op jit(solution)/shard_map/ppermute | solution.py:31
  (11 other events, 207.2 us)
Sparse Core Ops, SparseCore 0:
  21.4 50.1 all-gather.1

commit v3 on v2

--- a/solution.py
+++ b/solution.py
@@ -85,42 +85,38 @@
     heads_width = weights.shape[2]
     whole = heads_width // 256
 
-    def loads(n):
-        at = pl.ds(pl.multiple_of(n * 256, 256), 256) if n < whole else pl.ds(n * 256, 128)
-        to = 256 if n < whole else 128
-        return [
-            pltpu.make_async_copy(
-                weights.at[lax.rem(x + xr, XS), :, at], held.at[n, xr, :, :to], sems.at[n, xr]
-            )
-            for xr in range(XS)
-        ]
-
-    moves = [
-        copy for xr in range(XS) for copy in piece_copies(a_refs, b_refs, states, part_sems, xr)
-    ]
-    for copy in moves + [copy for n in range(whole + 1) for copy in loads(n)]:
-        copy.start()
-    for copy in moves:
+    def load(xr):
+        return pltpu.make_async_copy(weights.at[lax.rem(x + xr, XS)], held.at[xr], sems.at[xr])
+
+    moves = [piece_copies(a_refs, b_refs, states, part_sems, xr) for xr in range(XS)]
+    for xr in range(XS):
+        for copy in moves[xr]:
+            copy.start()
+        load(xr).start()
+
+    def columns(xr, first):
+        def add(at):
+            part = jnp.dot(states[xr], held[xr, :, at], preferred_element_type=f32)
+            pre[:, at] = part if first else pre[:, at] + part
+
+        @pl.loop(0, whole)
+        def _(n):
+            add(pl.ds(pl.multiple_of(n * 256, 256), 256))
+
+        if heads_width > whole * 256:
+            add(slice(whole * 256, heads_width))
+
+    for copy in moves[0]:
         copy.wait()
-
-    def columns(n, at, wide):
-        total = None
-        for xr in range(XS):
-            part = jnp.dot(states[xr], held[n, xr, :, :wide], preferred_element_type=f32)
-            total = part if xr == 0 else total + part
-        pre[:, at] = total
-
-    @pl.loop(0, whole)
-    def _(n):
-        for xr in range(XS):
-            pltpu.make_async_copy(
-                weights.at[xr, :, :256], held.at[n, xr], sems.at[n, xr]
-            ).wait()
-        columns(n, pl.ds(pl.multiple_of(n * 256, 256), 256), 256)
-
-    for copy in loads(whole):
+    load(0).wait()
+    columns(0, True)
+    for copy in sum(moves[1:], []):
         copy.wait()
-    columns(whole, slice(whole * 256, heads_width), heads_width - whole * 256)
+
+    @pl.loop(1, XS)
+    def _(xr):
+        load(xr).wait()
+        columns(xr, False)
 
 
 def score_kernel(place, pre, back, extras, said, kept, embed, sem):
@@ -285,11 +281,10 @@
                 preferred_element_type=f32,
             )
     value[...] = total
-    against(0)
     for load in sum(loads[1:], []):
         load.wait()
 
-    @pl.loop(1, XS)
+    @pl.loop(0, XS)
     def _(xr):
         against(xr)
 
@@ -409,8 +404,8 @@
         out_specs=vmem,
         scratch_shapes=[
             VMEM((XS, group, width), bf16),
-            VMEM((4 * cols // 256 + 1, XS, width, 256), bf16),
-            pltpu.SemaphoreType.DMA((4 * cols // 256 + 1, XS)),
+            VMEM((XS, width, 4 * cols), bf16),
+            pltpu.SemaphoreType.DMA((XS,)),
             pltpu.SemaphoreType.DMA((XS, YS, 2)),
         ],
         compiler_params=limit,

time: 189 us -> 189 us (level)
  no operation moved by 1% of the time
where the time goes in v3:
time: 189 us; the launch traced here: 188 us
  starting transfers between devices  76.6 us (41%)
  waiting for transfers between devices  50.3 us (27%)
  Pallas kernels  26.8 us (14%)
  between operations  15 us (8%)
  local copies, waits for them, and re-layouts  11.7 us (6%)
  other arithmetic  7.64 us (4%)
    ppermute x24, waiting for transfers between devices, ahead(): lax.ppermute(a, axis, tuple((((i + steps) % n, i) for i in range(n))))  43.3 us
    all_to_all x4, starting transfers between devices, exchange(): return lax.all_to_all(pieces, axes, split_axis=0, concat_axis=0, tiled=True)  38.5 us
    ppermute x24, starting transfers between devices, ahead(): lax.ppermute(a, axis, tuple((((i + steps) % n, i) for i in range(n))))  38.1 us
    pallas_call x1, Pallas kernels, on_device(): pl.pallas_call(forward_kernel, out_shape=jax.ShapeDtypeStruct((group, 4 *...  10.3 us
    pallas_call x1, Pallas kernels, on_device(): pl.pallas_call(backward_kernel, out_shape=(VMEM(packed, f32), VMEM(packed...  7.23 us
    all_to_all x4, waiting for transfers between devices, exchange(): return lax.all_to_all(pieces, axes, split_axis=0, concat_axis=0, tiled=True)  6.99 us
    pallas_call x1, Pallas kernels, on_device(): pl.pallas_call(score_kernel, out_shape=(jax.ShapeDtypeStruct((YS * XS, YS...  4.12 us
    gather x1, local copies, waits for them, and re-layouts, lookup(): found = table[got & 4095]  3.81 us
  transfers between devices with their start and end apart: 29, of which 10 were waited for; matrix products, arithmetic and copies ran while one was open for 7% of the time, Pallas kernels for 5%

profile of v3, /device:TPU:8, one launch (start us, length us, event | category | flops | bytes accessed | tf_op | source)
XLA Modules:
  0.0 188.3 jit_solution(17981429076944665962)
XLA Ops:
  7.8 2.2 %shard_map.162 = (bf16[56,896]{1,0:T(8,128)(2,1)}, bf16[56,896]{1,0:T(8,128)(2,1)}, bf16[56,896]{1,0:T(8,128)(2,1)}, bf16[56,896]{1,0:T(8,128)(2,1)}, bf16[64,896]{1,0:T(8,128)(2,1)}, /*index=5*/bf16[64,896]{1,0:T(8,128)(2,1)}) custom-call(s32[3]{0:T(128)} %pad_add_fusion.place, bf16[56,896]{1,0:T(8,128)(2,1)} %one.1, bf16[56,896]{1,0:T(8,128)(2,1)} %two.1, ...), custom_call_target="tpu_custom_call" | custom-call | tf_op jit(solution)/shard_map/pallas_call | solution.py:362
  10.0 2.2 %collective-permute-start.12 = (bf16[56,896]{1,0:T(8,128)(2,1)}, bf16[56,896]{1,0:T(8,128)(2,1)S(1)}, u32[]{:S(2)}, u32[]{:S(2)}) collective-permute-start(bf16[56,896]{1,0:T(8,128)(2,1)} %get-tuple-element.26), channel_id=1, source_target_pairs={{8,0},{16,8},{24,16},{0,24},{9,1},{17,9},{25,17},{1,25},{10,2},{18... | collective-permute-start | bytes 301064 | tf_op jit(solution)/shard_map/ppermute | solution.py:31
  13.1 1.9 %collective-permute-start.14 = (bf16[56,896]{1,0:T(8,128)(2,1)}, bf16[56,896]{1,0:T(8,128)(2,1)S(1)}, u32[]{:S(2)}, u32[]{:S(2)}) collective-permute-start(bf16[56,896]{1,0:T(8,128)(2,1)} %get-tuple-element.28), channel_id=1, source_target_pairs={{24,0},{0,8},{8,16},{16,24},{25,1},{1,9},{9,17},{17,25},{26,2},{2,... | collective-permute-start | bytes 301064 | tf_op jit(solution)/shard_map/ppermute | solution.py:31
  15.2 3.3 %collective-permute-done.13.refs_2_ = bf16[56,896]{1,0:T(8,128)(2,1)S(1)} collective-permute-done((bf16[56,896]{1,0:T(8,128)(2,1)}, bf16[56,896]{1,0:T(8,128)(2,1)S(1)}, u32[]{:S(2)}, u32[]{:S(2)}) %collective-permute-start.13) | collective-permute-done | bytes 100384 | tf_op jit(solution)/shard_map/ppermute | solution.py:31
  19.4 1.8 shard_map.163
  24.0 12.0 %all-to-all-start = ((s32[64,1,2]{2,1,0:T(1,128)}), s32[64,1,2]{2,1,0:T(1,128)S(1)}, u32[]{:S(2)}, u32[]{:S(2)}) async-start(s32[64,1,2]{2,1,0:T(1,128)} %bitcast.13), calls=%async_computation | async-start | bytes 65536 | tf_op jit(solution)/shard_map/all_to_all | solution.py:26
  36.0 1.5 collective-permute-start.8
  38.1 2.1 %collective-permute-start.7 = (bf16[64,896]{1,0:T(8,128)(2,1)}, bf16[64,896]{1,0:T(8,128)(2,1)S(1)}, u32[]{:S(2)}, u32[]{:S(2)}) collective-permute-start(bf16[64,896]{1,0:T(8,128)(2,1)} %get-tuple-element.24), channel_id=1, source_target_pairs={{16,0},{24,8},{0,16},{8,24},{17,1},{25,9},{1,17},{9,25},{18,2},{26... | collective-permute-start | bytes 344072 | tf_op jit(solution)/shard_map/ppermute | solution.py:31
  40.2 2.8 %collective-permute-start = (bf16[64,896]{1,0:T(8,128)(2,1)}, bf16[64,896]{1,0:T(8,128)(2,1)S(1)}, u32[]{:S(2)}, u32[]{:S(2)}) collective-permute-start(bf16[64,896]{1,0:T(8,128)(2,1)} %get-tuple-element.23), channel_id=1, source_target_pairs={{1,0},{2,1},{3,2},{0,3},{5,4},{6,5},{7,6},{4,7},{9,8},{10,9},{11,1... | collective-permute-start | bytes 344072 | tf_op jit(solution)/shard_map/ppermute | solution.py:31
  48.1 2.2 %collective-permute-start.10 = (bf16[4,64,896]{2,1,0:T(8,128)(2,1)S(1)}, bf16[4,64,896]{2,1,0:T(8,128)(2,1)S(1)}, u32[]{:S(2)}, u32[]{:S(2)}) collective-permute-start(bf16[4,64,896]{2,1,0:T(8,128)(2,1)S(1)} %pad_maximum_fusion.1.refs_4_), channel_id=1, source_target_pairs={{2,0},{3,1},{0,2},{1,3},{6,4},{7,5},{4,6},{5,7},{10,8},{11,9},{8,1... | collective-permute-start | bytes 1376264 | tf_op jit(solution)/shard_map/ppermute | solution.py:31
  50.5 1.2 collective-permute-start.11
  51.7 2.1 %collective-permute-start.9 = (bf16[4,64,896]{2,1,0:T(8,128)(2,1)S(1)}, bf16[4,64,896]{2,1,0:T(8,128)(2,1)S(1)}, u32[]{:S(2)}, u32[]{:S(2)}) collective-permute-start(bf16[4,64,896]{2,1,0:T(8,128)(2,1)S(1)} %pad_maximum_fusion.1.refs_4_), channel_id=1, source_target_pairs={{1,0},{2,1},{3,2},{0,3},{5,4},{6,5},{7,6},{4,7},{9,8},{10,9},{11,1... | collective-permute-start | bytes 1376264 | tf_op jit(solution)/shard_map/ppermute | solution.py:31
  53.8 7.6 %collective-permute-done.2 = bf16[64,896]{1,0:T(8,128)(2,1)S(1)} collective-permute-done((bf16[64,896]{1,0:T(8,128)(2,1)}, bf16[64,896]{1,0:T(8,128)(2,1)S(1)}, u32[]{:S(2)}, u32[]{:S(2)}) %collective-permute-start.2) | collective-permute-done | bytes 114720 | tf_op jit(solution)/shard_map/ppermute | solution.py:31
  62.4 1.5 collective-permute-start.3
  65.1 1.6 collective-permute-start.5
  66.7 3.8 %gather_fusion = bf16[128,896]{1,0:T(8,128)(2,1)S(1)} fusion(bf16[2376,896]{1,0:T(8,128)(2,1)} %param.15, s32[1024]{0:T(1024)S(1)} %pad_clamp_fusion), kind=kCustom, calls=%fused_computation | custom fusion | bytes 459264 | tf_op jit(solution)/shard_map/gather | solution.py:332
  72.8 10.6 %all-to-all-start.1 = ((bf16[64,8,225]{2,1,0:T(8,128)(2,1)}), bf16[64,8,225]{2,1,0:T(8,128)(2,1)S(1)}, u32[]{:S(2)}, u32[]{:S(2)}) async-start(bf16[64,8,225]{2,1,0:T(8,128)(2,1)} %reshape.176), calls=%async_computation.1 | async-start | bytes 524288 | tf_op jit(solution)/shard_map/all_to_all | solution.py:26
  84.7 10.3 %shard_map.164.pre = f32[512,896]{1,0:T(8,128)S(1)} custom-call(s32[3]{0:T(128)S(1)} %copy-done, bf16[4,64,896]{2,1,0:T(8,128)(2,1)} %copy-done.3, bf16[4,64,896]{2,1,0:T(8,128)(2,1)} %collective-permute-done.3.refs_1_, bf16[4,64,896]{2,1,0:T(8,128)(2,1)} %collective-permute-done.4.refs_2_, bf16[4,64,896]{2,1,0:T(8,128)(2,1)} %collective-permute-done.5.refs_3_, ...), custom_call_target="tpu_custom_call" | custom-call | flops 3288334336 | bytes 12582912 | tf_op jit(solution)/shard_map/pallas_call | solution.py:400
  95.7 4.1 %shard_map.165 = (f32[16,4,8,128]{3,2,1,0:T(8,128)}, bf16[512,512]{1,0:T(8,128)(2,1)}) custom-call(s32[3]{0:T(128)S(1)} %copy-done, f32[512,896]{1,0:T(8,128)S(1)} %shard_map.164.pre, bf16[512,225]{1,0:T(8,128)(2,1)S(1)} %bitcast.41, f32[8,128]{1,0:T(8,128)S(1)} %concatenate.10.extras), custom_call_target="tpu_custom_call" | custom-call | tf_op jit(solution)/shard_map/pallas_call | solution.py:416
  99.8 6.8 %all-to-all-start.2 = ((f32[16,4,8,128]{3,2,1,0:T(8,128)}), f32[16,4,8,128]{3,2,1,0:T(8,128)S(1)}, u32[]{:S(2)}, u32[]{:S(2)}) async-start(f32[16,4,8,128]{3,2,1,0:T(8,128)} %get-tuple-element.29), calls=%async_computation.2 | async-start | bytes 524288 | tf_op jit(solution)/shard_map/all_to_all | solution.py:26
  107.2 6.3 %all-to-all-done.2 = f32[16,4,8,128]{3,2,1,0:T(8,128)S(1)} async-done(((f32[16,4,8,128]{3,2,1,0:T(8,128)}), f32[16,4,8,128]{3,2,1,0:T(8,128)S(1)}, u32[]{:S(2)}, u32[]{:S(2)}) %all-to-all-start.2) | async-done | bytes 262176 | tf_op jit(solution)/shard_map/all_to_all | solution.py:26
  113.6 7.2 %shard_map.166 = (f32[8,4,200,128]{3,2,1,0:T(8,128)S(1)}, bf16[8,4,200,128]{3,2,1,0:T(8,128)(2,1)S(1)}, f32[8,128]{1,0:T(8,128)S(1)}, f32[8,896]{1,0:T(8,128)S(1)}) custom-call(s32[3]{0:T(128)S(1)} %copy-done, f32[1]{0:T(128)S(6)} %copy.51.bias, f32[4,4,4,8,128]{4,3,2,1,0:T(8,128)S(1)} %bitcast.42, f32[512,896]{1,0:T(8,128)S(1)} %shard_map.164.pre, ...), custom_call_target="tpu_custom_call" | custom-call | flops 1879048192 | bytes 12582912 | tf_op jit(solution)/shard_map/pallas_call | solution.py:430
  120.9 3.5 %collective-permute-done.23 = bf16[8,4,200,128]{3,2,1,0:T(8,128)(2,1)S(1)} collective-permute-done((bf16[8,4,200,128]{3,2,1,0:T(8,128)(2,1)S(1)}, bf16[8,4,200,128]{3,2,1,0:T(8,128)(2,1)S(1)}, u32[]{:S(2)}, u32[]{:S(2)}) %collective-permute-start.23) | collective-permute-done | bytes 1638432 | tf_op jit(solution)/shard_map/ppermute | solution.py:31
  124.4 1.6 add_convert_fusion
  126.0 9.1 %all-to-all-start.3 = ((bf16[32,200,128]{2,1,0:T(8,128)(2,1)}), bf16[32,200,128]{2,1,0:T(8,128)(2,1)S(1)}, u32[]{:S(2)}, u32[]{:S(2)}) async-start(bf16[32,200,128]{2,1,0:T(8,128)(2,1)} %bitcast.25), calls=%async_computation.3 | async-start | bytes 3276800 | tf_op jit(solution)/shard_map/all_to_all | solution.py:26
  136.6 2.8 %collective-permute-start.16 = (f32[10,128]{1,0:T(8,128)S(1)}, f32[10,128]{1,0:T(8,128)S(1)}, u32[]{:S(2)}, u32[]{:S(2)}) collective-permute-start(f32[10,128]{1,0:T(8,128)S(1)} %fusion.3.refs_0_), channel_id=1, source_target_pairs={{32,0},{64,32},{96,64},{128,96},{160,128},{192,160},{224,192},{0,2... | collective-permute-start | bytes 15368 | tf_op jit(solution)/shard_map/ppermute | solution.py:31
  139.4 2.3 %collective-permute-start.17 = (f32[10,128]{1,0:T(8,128)S(1)}, f32[10,128]{1,0:T(8,128)S(1)}, u32[]{:S(2)}, u32[]{:S(2)}) collective-permute-start(f32[10,128]{1,0:T(8,128)S(1)} %fusion.3.refs_0_), channel_id=1, source_target_pairs={{64,0},{96,32},{128,64},{160,96},{192,128},{224,160},{0,192},{32,2... | collective-permute-start | bytes 15368 | tf_op jit(solution)/shard_map/ppermute | solution.py:31
  141.7 1.4 collective-permute-start.18
  143.1 3.6 %collective-permute-start.19 = (f32[10,128]{1,0:T(8,128)S(1)}, f32[10,128]{1,0:T(8,128)S(1)}, u32[]{:S(2)}, u32[]{:S(2)}) collective-permute-start(f32[10,128]{1,0:T(8,128)S(1)} %fusion.3.refs_0_), channel_id=1, source_target_pairs={{128,0},{160,32},{192,64},{224,96},{0,128},{32,160},{64,192},{96,2... | collective-permute-start | bytes 15368 | tf_op jit(solution)/shard_map/ppermute | solution.py:31
  146.9 26.4 %collective-permute-done.16.refs_1_ = f32[10,128]{1,0:T(8,128)S(1)} collective-permute-done((f32[10,128]{1,0:T(8,128)S(1)}, f32[10,128]{1,0:T(8,128)S(1)}, u32[]{:S(2)}, u32[]{:S(2)}) %collective-permute-start.16) | collective-permute-done | bytes 5152 | tf_op jit(solution)/shard_map/ppermute | solution.py:31
  173.3 4.2 %collective-permute-start.22 = (f32[10,128]{1,0:T(8,128)S(1)}, f32[10,128]{1,0:T(8,128)S(1)}, u32[]{:S(2)}, u32[]{:S(2)}) collective-permute-start(f32[10,128]{1,0:T(8,128)S(1)} %fusion.3.refs_0_), channel_id=1, source_target_pairs={{224,0},{0,32},{32,64},{64,96},{96,128},{128,160},{160,192},{192,2... | collective-permute-start | bytes 15368 | tf_op jit(solution)/shard_map/ppermute | solution.py:31
  180.2 1.3 fusion.4
  (107 shorter events, 21.9 us)
Async XLA Ops:
  7.2 76.6 %all-gather.2.cloned.1.call-start = ((), (), s32[]{:S(2)}) async-start(), calls=%async_computation.4 | async-start | bytes 6823936 | tf_op jit(solution)/shard_map/all_gather | solution.py:376
  10.0 5.2 %collective-permute-start.12 = (bf16[56,896]{1,0:T(8,128)(2,1)}, bf16[56,896]{1,0:T(8,128)(2,1)S(1)}, u32[]{:S(2)}, u32[]{:S(2)}) collective-permute-start(bf16[56,896]{1,0:T(8,128)(2,1)} %get-tuple-element.26), channel_id=1, source_target_pairs={{8,0},{16,8},{24,16},{0,24},{9,1},{17,9},{25,17},{1,25},{10,2},{18... | collective-permute-start | bytes 301064 | tf_op jit(solution)/shard_map/ppermute | solution.py:31
  12.2 6.4 %collective-permute-start.13 = (bf16[56,896]{1,0:T(8,128)(2,1)}, bf16[56,896]{1,0:T(8,128)(2,1)S(1)}, u32[]{:S(2)}, u32[]{:S(2)}) collective-permute-start(bf16[56,896]{1,0:T(8,128)(2,1)} %get-tuple-element.27), channel_id=1, source_target_pairs={{16,0},{24,8},{0,16},{8,24},{17,1},{25,9},{1,17},{9,25},{18,2},{26... | collective-permute-start | bytes 301064 | tf_op jit(solution)/shard_map/ppermute | solution.py:31
  13.1 5.7 %collective-permute-start.14 = (bf16[56,896]{1,0:T(8,128)(2,1)}, bf16[56,896]{1,0:T(8,128)(2,1)S(1)}, u32[]{:S(2)}, u32[]{:S(2)}) collective-permute-start(bf16[56,896]{1,0:T(8,128)(2,1)} %get-tuple-element.28), channel_id=1, source_target_pairs={{24,0},{0,8},{8,16},{16,24},{25,1},{1,9},{9,17},{17,25},{26,2},{2,... | collective-permute-start | bytes 301064 | tf_op jit(solution)/shard_map/ppermute | solution.py:31
  24.0 22.0 %all-to-all-start = ((s32[64,1,2]{2,1,0:T(1,128)}), s32[64,1,2]{2,1,0:T(1,128)S(1)}, u32[]{:S(2)}, u32[]{:S(2)}) async-start(s32[64,1,2]{2,1,0:T(1,128)} %bitcast.13), calls=%async_computation | async-start | bytes 65536 | tf_op jit(solution)/shard_map/all_to_all | solution.py:26
  36.0 10.1 %collective-permute-start.8 = (bf16[64,896]{1,0:T(8,128)(2,1)}, bf16[64,896]{1,0:T(8,128)(2,1)S(1)}, u32[]{:S(2)}, u32[]{:S(2)}) collective-permute-start(bf16[64,896]{1,0:T(8,128)(2,1)} %get-tuple-element.24), channel_id=1, source_target_pairs={{24,0},{0,8},{8,16},{16,24},{25,1},{1,9},{9,17},{17,25},{26,2},{2,... | collective-permute-start | bytes 344072 | tf_op jit(solution)/shard_map/ppermute | solution.py:31
  37.6 9.5 %collective-permute-start.6 = (bf16[64,896]{1,0:T(8,128)(2,1)}, bf16[64,896]{1,0:T(8,128)(2,1)S(1)}, u32[]{:S(2)}, u32[]{:S(2)}) collective-permute-start(bf16[64,896]{1,0:T(8,128)(2,1)} %get-tuple-element.24), channel_id=1, source_target_pairs={{8,0},{16,8},{24,16},{0,24},{9,1},{17,9},{25,17},{1,25},{10,2},{18... | collective-permute-start | bytes 344072 | tf_op jit(solution)/shard_map/ppermute | solution.py:31
  38.1 9.0 %collective-permute-start.7 = (bf16[64,896]{1,0:T(8,128)(2,1)}, bf16[64,896]{1,0:T(8,128)(2,1)S(1)}, u32[]{:S(2)}, u32[]{:S(2)}) collective-permute-start(bf16[64,896]{1,0:T(8,128)(2,1)} %get-tuple-element.24), channel_id=1, source_target_pairs={{16,0},{24,8},{0,16},{8,24},{17,1},{25,9},{1,17},{9,25},{18,2},{26... | collective-permute-start | bytes 344072 | tf_op jit(solution)/shard_map/ppermute | solution.py:31
  40.2 11.5 %collective-permute-start = (bf16[64,896]{1,0:T(8,128)(2,1)}, bf16[64,896]{1,0:T(8,128)(2,1)S(1)}, u32[]{:S(2)}, u32[]{:S(2)}) collective-permute-start(bf16[64,896]{1,0:T(8,128)(2,1)} %get-tuple-element.23), channel_id=1, source_target_pairs={{1,0},{2,1},{3,2},{0,3},{5,4},{6,5},{7,6},{4,7},{9,8},{10,9},{11,1... | collective-permute-start | bytes 344072 | tf_op jit(solution)/shard_map/ppermute | solution.py:31
  42.9 10.9 %collective-permute-start.1 = (bf16[64,896]{1,0:T(8,128)(2,1)}, bf16[64,896]{1,0:T(8,128)(2,1)S(1)}, u32[]{:S(2)}, u32[]{:S(2)}) collective-permute-start(bf16[64,896]{1,0:T(8,128)(2,1)} %get-tuple-element.23), channel_id=1, source_target_pairs={{2,0},{3,1},{0,2},{1,3},{6,4},{7,5},{4,6},{5,7},{10,8},{11,9},{8,1... | collective-permute-start | bytes 344072 | tf_op jit(solution)/shard_map/ppermute | solution.py:31
  46.1 15.3 %collective-permute-start.2 = (bf16[64,896]{1,0:T(8,128)(2,1)}, bf16[64,896]{1,0:T(8,128)(2,1)S(1)}, u32[]{:S(2)}, u32[]{:S(2)}) collective-permute-start(bf16[64,896]{1,0:T(8,128)(2,1)} %get-tuple-element.23), channel_id=1, source_target_pairs={{3,0},{0,1},{1,2},{2,3},{7,4},{4,5},{5,6},{6,7},{11,8},{8,9},{9,10... | collective-permute-start | bytes 344072 | tf_op jit(solution)/shard_map/ppermute | solution.py:31
  48.1 17.0 %collective-permute-start.10 = (bf16[4,64,896]{2,1,0:T(8,128)(2,1)S(1)}, bf16[4,64,896]{2,1,0:T(8,128)(2,1)S(1)}, u32[]{:S(2)}, u32[]{:S(2)}) collective-permute-start(bf16[4,64,896]{2,1,0:T(8,128)(2,1)S(1)} %pad_maximum_fusion.1.refs_4_), channel_id=1, source_target_pairs={{2,0},{3,1},{0,2},{1,3},{6,4},{7,5},{4,6},{5,7},{10,8},{11,9},{8,1... | collective-permute-start | bytes 1376264 | tf_op jit(solution)/shard_map/ppermute | solution.py:31
  50.5 33.2 %collective-permute-start.11 = (bf16[4,64,896]{2,1,0:T(8,128)(2,1)S(1)}, bf16[4,64,896]{2,1,0:T(8,128)(2,1)S(1)}, u32[]{:S(2)}, u32[]{:S(2)}) collective-permute-start(bf16[4,64,896]{2,1,0:T(8,128)(2,1)S(1)} %pad_maximum_fusion.1.refs_4_), channel_id=1, source_target_pairs={{3,0},{0,1},{1,2},{2,3},{7,4},{4,5},{5,6},{6,7},{11,8},{8,9},{9,10... | collective-permute-start | bytes 1376264 | tf_op jit(solution)/shard_map/ppermute | solution.py:31
  51.7 32.0 %collective-permute-start.9 = (bf16[4,64,896]{2,1,0:T(8,128)(2,1)S(1)}, bf16[4,64,896]{2,1,0:T(8,128)(2,1)S(1)}, u32[]{:S(2)}, u32[]{:S(2)}) collective-permute-start(bf16[4,64,896]{2,1,0:T(8,128)(2,1)S(1)} %pad_maximum_fusion.1.refs_4_), channel_id=1, source_target_pairs={{1,0},{2,1},{3,2},{0,3},{5,4},{6,5},{7,6},{4,7},{9,8},{10,9},{11,1... | collective-permute-start | bytes 1376264 | tf_op jit(solution)/shard_map/ppermute | solution.py:31
  62.4 21.4 %collective-permute-start.3 = (bf16[4,64,896]{2,1,0:T(8,128)(2,1)S(1)}, bf16[4,64,896]{2,1,0:T(8,128)(2,1)}, u32[]{:S(2)}, u32[]{:S(2)}) collective-permute-start(bf16[4,64,896]{2,1,0:T(8,128)(2,1)S(1)} %pad_maximum_fusion.refs_0_), channel_id=1, source_target_pairs={{8,0},{16,8},{24,16},{0,24},{9,1},{17,9},{25,17},{1,25},{10,2},{18... | collective-permute-start | bytes 1376264 | tf_op jit(solution)/shard_map/ppermute | solution.py:31
  63.9 19.9 %collective-permute-start.4 = (bf16[4,64,896]{2,1,0:T(8,128)(2,1)S(1)}, bf16[4,64,896]{2,1,0:T(8,128)(2,1)}, u32[]{:S(2)}, u32[]{:S(2)}) collective-permute-start(bf16[4,64,896]{2,1,0:T(8,128)(2,1)S(1)} %pad_maximum_fusion.refs_0_), channel_id=1, source_target_pairs={{16,0},{24,8},{0,16},{8,24},{17,1},{25,9},{1,17},{9,25},{18,2},{26... | collective-permute-start | bytes 1376264 | tf_op jit(solution)/shard_map/ppermute | solution.py:31
  65.1 18.7 %collective-permute-start.5 = (bf16[4,64,896]{2,1,0:T(8,128)(2,1)S(1)}, bf16[4,64,896]{2,1,0:T(8,128)(2,1)}, u32[]{:S(2)}, u32[]{:S(2)}) collective-permute-start(bf16[4,64,896]{2,1,0:T(8,128)(2,1)S(1)} %pad_maximum_fusion.refs_0_), channel_id=1, source_target_pairs={{24,0},{0,8},{8,16},{16,24},{25,1},{1,9},{9,17},{17,25},{26,2},{2,... | collective-permute-start | bytes 1376264 | tf_op jit(solution)/shard_map/ppermute | solution.py:31
  72.8 22.8 %all-to-all-start.1 = ((bf16[64,8,225]{2,1,0:T(8,128)(2,1)}), bf16[64,8,225]{2,1,0:T(8,128)(2,1)S(1)}, u32[]{:S(2)}, u32[]{:S(2)}) async-start(bf16[64,8,225]{2,1,0:T(8,128)(2,1)} %reshape.176), calls=%async_computation.1 | async-start | bytes 524288 | tf_op jit(solution)/shard_map/all_to_all | solution.py:26
  99.8 13.8 %all-to-all-start.2 = ((f32[16,4,8,128]{3,2,1,0:T(8,128)}), f32[16,4,8,128]{3,2,1,0:T(8,128)S(1)}, u32[]{:S(2)}, u32[]{:S(2)}) async-start(f32[16,4,8,128]{3,2,1,0:T(8,128)} %get-tuple-element.29), calls=%async_computation.2 | async-start | bytes 524288 | tf_op jit(solution)/shard_map/all_to_all | solution.py:26
  120.8 3.6 %collective-permute-start.23 = (bf16[8,4,200,128]{3,2,1,0:T(8,128)(2,1)S(1)}, bf16[8,4,200,128]{3,2,1,0:T(8,128)(2,1)S(1)}, u32[]{:S(2)}, u32[]{:S(2)}) collective-permute-start(bf16[8,4,200,128]{3,2,1,0:T(8,128)(2,1)S(1)} %get-tuple-element.34), channel_id=1, source_target_pairs={{4,0},{0,4},{5,1},{1,5},{6,2},{2,6},{7,3},{3,7},{12,8},{8,12},{13,... | collective-permute-start | bytes 4915208 | tf_op jit(solution)/shard_map/ppermute | solution.py:31
  126.0 51.5 %copy-start.5 = (bf16[56,896]{1,0:T(8,128)(2,1)S(1)}, bf16[56,896]{1,0:T(8,128)(2,1)}, u32[]{:S(2)}) copy-start(bf16[56,896]{1,0:T(8,128)(2,1)} %two.1) | copy-start | bytes 301060
  126.0 51.5 %copy-start.6 = (bf16[56,896]{1,0:T(8,128)(2,1)S(1)}, bf16[56,896]{1,0:T(8,128)(2,1)}, u32[]{:S(2)}) copy-start(bf16[56,896]{1,0:T(8,128)(2,1)} %three.1) | copy-start | bytes 301060
  126.0 51.5 %copy-start.7 = (bf16[56,896]{1,0:T(8,128)(2,1)S(1)}, bf16[56,896]{1,0:T(8,128)(2,1)}, u32[]{:S(2)}) copy-start(bf16[56,896]{1,0:T(8,128)(2,1)} %four.1) | copy-start | bytes 301060
  126.0 53.1 %all-to-all-start.3 = ((bf16[32,200,128]{2,1,0:T(8,128)(2,1)}), bf16[32,200,128]{2,1,0:T(8,128)(2,1)S(1)}, u32[]{:S(2)}, u32[]{:S(2)}) async-start(bf16[32,200,128]{2,1,0:T(8,128)(2,1)} %bitcast.25), calls=%async_computation.3 | async-start | bytes 3276800 | tf_op jit(solution)/shard_map/all_to_all | solution.py:26
  135.3 1.3 collective-permute-start.15
  136.6 36.7 %collective-permute-start.16 = (f32[10,128]{1,0:T(8,128)S(1)}, f32[10,128]{1,0:T(8,128)S(1)}, u32[]{:S(2)}, u32[]{:S(2)}) collective-permute-start(f32[10,128]{1,0:T(8,128)S(1)} %fusion.3.refs_0_), channel_id=1, source_target_pairs={{32,0},{64,32},{96,64},{128,96},{160,128},{192,160},{224,192},{0,2... | collective-permute-start | bytes 15368 | tf_op jit(solution)/shard_map/ppermute | solution.py:31
  139.4 34.0 %collective-permute-start.17 = (f32[10,128]{1,0:T(8,128)S(1)}, f32[10,128]{1,0:T(8,128)S(1)}, u32[]{:S(2)}, u32[]{:S(2)}) collective-permute-start(f32[10,128]{1,0:T(8,128)S(1)} %fusion.3.refs_0_), channel_id=1, source_target_pairs={{64,0},{96,32},{128,64},{160,96},{192,128},{224,160},{0,192},{32,2... | collective-permute-start | bytes 15368 | tf_op jit(solution)/shard_map/ppermute | solution.py:31
  141.7 36.6 %collective-permute-start.18 = (f32[10,128]{1,0:T(8,128)S(1)}, f32[10,128]{1,0:T(8,128)S(1)}, u32[]{:S(2)}, u32[]{:S(2)}) collective-permute-start(f32[10,128]{1,0:T(8,128)S(1)} %fusion.3.refs_0_), channel_id=1, source_target_pairs={{96,0},{128,32},{160,64},{192,96},{224,128},{0,160},{32,192},{64,2... | collective-permute-start | bytes 15368 | tf_op jit(solution)/shard_map/ppermute | solution.py:31
  143.1 35.2 %collective-permute-start.19 = (f32[10,128]{1,0:T(8,128)S(1)}, f32[10,128]{1,0:T(8,128)S(1)}, u32[]{:S(2)}, u32[]{:S(2)}) collective-permute-start(f32[10,128]{1,0:T(8,128)S(1)} %fusion.3.refs_0_), channel_id=1, source_target_pairs={{128,0},{160,32},{192,64},{224,96},{0,128},{32,160},{64,192},{96,2... | collective-permute-start | bytes 15368 | tf_op jit(solution)/shard_map/ppermute | solution.py:31
  146.7 31.5 %collective-permute-start.20 = (f32[10,128]{1,0:T(8,128)S(1)}, f32[10,128]{1,0:T(8,128)S(1)}, u32[]{:S(2)}, u32[]{:S(2)}) collective-permute-start(f32[10,128]{1,0:T(8,128)S(1)} %fusion.3.refs_0_), channel_id=1, source_target_pairs={{160,0},{192,32},{224,64},{0,96},{32,128},{64,160},{96,192},{128,2... | collective-permute-start | bytes 15368 | tf_op jit(solution)/shard_map/ppermute | solution.py:31
  173.3 5.8 %collective-permute-start.21 = (f32[10,128]{1,0:T(8,128)S(1)}, f32[10,128]{1,0:T(8,128)S(1)}, u32[]{:S(2)}, u32[]{:S(2)}) collective-permute-start(f32[10,128]{1,0:T(8,128)S(1)} %fusion.3.refs_0_), channel_id=1, source_target_pairs={{192,0},{224,32},{0,64},{32,96},{64,128},{96,160},{128,192},{160,2... | collective-permute-start | bytes 15368 | tf_op jit(solution)/shard_map/ppermute | solution.py:31
  173.3 5.8 %collective-permute-start.22 = (f32[10,128]{1,0:T(8,128)S(1)}, f32[10,128]{1,0:T(8,128)S(1)}, u32[]{:S(2)}, u32[]{:S(2)}) collective-permute-start(f32[10,128]{1,0:T(8,128)S(1)} %fusion.3.refs_0_), channel_id=1, source_target_pairs={{224,0},{0,32},{32,64},{64,96},{96,128},{128,160},{160,192},{192,2... | collective-permute-start | bytes 15368 | tf_op jit(solution)/shard_map/ppermute | solution.py:31
  (11 other events, 207.8 us)
Sparse Core Ops, SparseCore 0:
  21.4 50.1 all-gather.1
